TPU v7x, 512 devices: a 8x2x16 block of a 8x8x16 slice. The times are simulated.
512 devices in a mesh: subj: 2 (over y), row: 16 (over x, core), col: 16 (over z).
Axes of the slice: x: 8, y: 2, z: 16, core: 2. Of those that a mesh axis runs over, the one named last changes fastest.
The devices are a block of a 8x8x16 slice.
Arguments:
- series: float32 [800, 65536], P(None, ('subj', 'row', 'col')), parts along dimension 1, as said below
- keep_mask: int32 [512, 256], P(('subj', 'row'), 'col'), parts along dimension 0, may hold values from 0 to 1, as said below
- row_owner: int32 [512], P('subj'), parts along dimension 0, may hold values from 0 to 15, as said below
Outputs:
- owned_tiles: bfloat16 [32, 16, 96, 128, 128], P(('subj', 'row'), 'col'), parts along dimension 0
- owned_ids: int32 [32, 16, 96], P(('subj', 'row'), 'col'), parts along dimension 0
There are 2 independent parts, one for each index of `subj`. A program takes and returns all parts, laid end to end along the dimension named above; each array names one. Nothing has to cross between parts.
Inputs may be any that keep to these rules, and one draw needn't show every extreme that they name: Each voxel's series varies over time. `keep_mask`: of the 16 tiles that one tile row has in one column block, at most 6 are kept; in every draw one owner keeps exactly 6 in each of its tile rows in some column block. `row_owner`: the 16 tile rows of a row block have 16 different owners, and every owner holds 16 tile rows, from 16 different row blocks.
All inputs are finite; a program needn't handle non-finite values.
Results may differ from a plain program's by a relative error of at most 0.0042.
Values may be sent and summed in bfloat16 or wider, within the bound.
No kernel may reach another device: no remote copies, remote signals or barrier semaphores. Data moves between devices by JAX's collectives and lax.ppermute only.
A program may use at most 64 MiB of HBM per device.

v0:
```python
import jax
import jax.numpy as jnp
from jax import lax
from jax.sharding import PartitionSpec as P

TILE = 128


epsilon = 1e-05


def compact(flat_tiles, flat_ids, capacity):
    is_valid = (flat_ids >= 0).astype(jnp.int32)
    running = jnp.cumsum(is_valid)
    slot_index = jnp.arange(capacity, dtype=jnp.int32)
    position = jnp.arange(flat_ids.shape[0], dtype=jnp.int32)
    slot_hit = (is_valid[None, :] == 1) & (running[None, :] == slot_index[:, None] + 1)
    picked = jnp.sum(jnp.where(slot_hit, position[None, :], 0), axis=1)
    present = running[-1] > slot_index
    chosen = jnp.take(flat_tiles, picked, axis=0)
    slot_tiles = jnp.where(present[:, None, None], chosen, jnp.zeros_like(chosen))
    slot_ids = jnp.where(present, jnp.take(flat_ids, picked), -1).astype(jnp.int32)
    return (slot_tiles, slot_ids)


def shards(series, keep_mask, row_owner):
    frames = series.shape[0]
    average = jnp.mean(series, axis=0, keepdims=True)
    centred = series - average
    spread = jnp.mean(centred * centred, axis=0, keepdims=True)
    scored = (centred * lax.rsqrt(spread + epsilon)).astype(jnp.bfloat16)
    row_block = lax.all_gather(scored, "col", axis=1, tiled=True)
    product = lax.dot_general(
        row_block,
        lax.all_gather(scored, "row", axis=1, tiled=True),
        (((0,), (0,)), ((), ())),
        preferred_element_type=jnp.float32,
    )
    tile_grid = (product * (1.0 / frames)).astype(jnp.bfloat16)
    row_count, col_count = keep_mask.shape
    tile_grid = tile_grid.reshape(row_count, TILE, col_count, TILE).transpose(0, 2, 1, 3)
    row_devices = lax.axis_size("row")
    col_devices = lax.axis_size("col")
    row_index = lax.axis_index("row")
    col_index = lax.axis_index("col")
    total_cols = col_count * col_devices
    slot_limit = max(2, 3 * col_count // 8)
    capacity = row_count * slot_limit
    local_owner = lax.dynamic_slice_in_dim(row_owner, row_index * row_count, row_count)
    targets = jnp.arange(row_devices, dtype=jnp.int32)
    owns_row = local_owner[None, :] == targets[:, None]
    has_row = jnp.any(owns_row, axis=1)
    row_of = jnp.sum(
        jnp.where(owns_row, jnp.arange(row_count, dtype=jnp.int32)[None, :], 0), axis=1
    )
    keep_flags = jnp.where(has_row[:, None], jnp.take(keep_mask, row_of, axis=0), 0)
    global_row = row_index * row_count + row_of
    first_col = col_index * col_count
    running = jnp.cumsum(keep_flags, axis=1)
    slot_index = jnp.arange(slot_limit, dtype=jnp.int32)
    slot_hit = (keep_flags[:, None, :] == 1) & (
        running[:, None, :] == slot_index[None, :, None] + 1
    )
    picked = jnp.sum(
        jnp.where(slot_hit, jnp.arange(col_count, dtype=jnp.int32)[None, None, :], 0), axis=2
    )
    present = running[:, -1:] > slot_index[None, :]
    chosen = tile_grid[row_of[:, None], picked]
    outgoing = jnp.where(present[:, :, None, None], chosen, jnp.zeros_like(chosen))
    out_ids = jnp.where(present, global_row[:, None] * total_cols + first_col + picked, -1)
    incoming, in_ids = (
        lax.all_to_all(outgoing, "row", split_axis=0, concat_axis=0, tiled=True),
        lax.all_to_all(out_ids, "row", split_axis=0, concat_axis=0, tiled=True),
    )
    flat_tiles = incoming.reshape(-1, TILE, TILE)
    flat_ids = in_ids.reshape(-1)
    slot_tiles, slot_ids = compact(flat_tiles, flat_ids, capacity)
    return (slot_tiles.reshape(1, 1, capacity, TILE, TILE), slot_ids.reshape(1, 1, capacity))


def solution(mesh):
    in_specs = (P(None, ("subj", "row", "col")), P(("subj", "row"), "col"), P("subj"))
    out_specs = (P(("subj", "row"), "col", None, None, None), P(("subj", "row"), "col", None))
    return jax.shard_map(shards, mesh=mesh, in_specs=in_specs, out_specs=out_specs, check_vma=False)
```

profile of v0, /device:TPU:65, one launch (start us, length us, event | category | flops | bytes accessed | tf_op | source)
XLA Modules:
  0.0 313.3 jit_solution(12894685114126903149)
XLA Ops:
  7.3 1.1 reduce_sum.60
  8.4 1.1 multiply_reduce_fusion
  9.5 1.7 multiply_convert_fusion.1
  11.4 0.7 all-gather.5.cloned.1.call-update
  12.1 0.8 dynamic_slice.3
  13.0 0.6 gather_fusion
  14.4 0.7 copy.18
  15.1 44.6 %all-to-all-start = ((s32[16,1,6]{2,1,0:T(1,128)}), s32[16,1,6]{2,1,0:T(1,128)S(1)}, u32[]{:S(2)}, u32[]{:S(2)}) async-start(s32[16,1,6]{2,1,0:T(1,128)} %copy.18), calls=%async_computation | async-start | bytes 16384 | tf_op jit(solution)/shard_map/all_to_all | solution.py:73
  60.0 64.0 %all-gather.3.cloned.1.call-done = bf16[800,2048]{1,0:T(8,128)(2,1)} async-done(((bf16[800,128]{1,0:T(8,128)(2,1)}), bf16[800,2048]{1,0:T(8,128)(2,1)}) %all-gather.3.cloned.1.call-update) | async-done | bytes 3276816 | tf_op jit(solution)/shard_map/all_gather | solution.py:32
  124.0 61.5 %all-gather.5.cloned.1.call-done = bf16[800,2048]{1,0:T(8,128)(2,1)} async-done(((bf16[800,128]{1,0:T(8,128)(2,1)}), bf16[800,2048]{1,0:T(8,128)(2,1)}) %all-gather.5.cloned.1.call-update) | async-done | bytes 3276816 | tf_op jit(solution)/shard_map/all_gather | solution.py:35
  185.5 13.6 %fusion = bf16[256,8,16,128]{3,1,2,0:T(8,128)(2,1)} fusion(bf16[800,2048]{1,0:T(8,128)(2,1)} %all-gather.3.cloned.1.call-done, bf16[800,2048]{1,0:T(8,128)(2,1)} %all-gather.5.cloned.1.call-done), kind=kOutput, calls=%fused_computation.6 | convolution fusion | flops 6719275008 | bytes 14942208 | tf_op jit(solution)/shard_map/dot_general | solution.py:33
  199.2 9.7 %copy.22 = bf16[256,8,16,128]{3,2,1,0:T(8,128)(2,1)} copy(bf16[256,8,16,128]{3,1,2,0:T(8,128)(2,1)} %fusion) | data formatting | bytes 16777216
  208.9 9.1 %copy.24 = bf16[16,128,16,128]{3,1,2,0:T(8,128)(2,1)} copy(bf16[16,128,16,128]{3,2,1,0:T(8,128)(2,1)} %bitcast.36) | data formatting | bytes 16777216 | tf_op jit(solution)/shard_map/reshape | solution.py:41
  218.0 4.9 %gather_fusion.1 = bf16[96,128,128]{2,1,0:T(8,128)(2,1)S(1)} fusion(bf16[16,16,128,128]{3,2,1,0:T(8,128)(2,1)} %bitcast.37, s32[96]{0:T(128)S(1)} %reshape.311), kind=kCustom, calls=%fused_computation.1 | custom fusion | bytes 6292224 | tf_op jit(solution)/shard_map/gather | solution.py:68
  223.0 1.9 broadcast_select_fusion
  224.9 4.5 %all-to-all-start.1 = ((bf16[16,6,128,128]{3,2,1,0:T(8,128)(2,1)}), bf16[16,6,128,128]{3,2,1,0:T(8,128)(2,1)S(1)}, u32[]{:S(2)}, u32[]{:S(2)}) async-start(bf16[16,6,128,128]{3,2,1,0:T(8,128)(2,1)} %broadcast_select_fusion), calls=%async_computation.1 | async-start | bytes 6291456 | tf_op jit(solution)/shard_map/all_to_all | solution.py:72
  229.9 0.7 fusion.11
  230.9 0.6 slice.21
  231.8 1.2 gather_fusion.3
  233.1 0.7 compare_and_fusion
  233.8 1.2 compare_select_fusion.6
  235.0 65.3 %all-to-all-done.1 = bf16[16,6,128,128]{3,2,1,0:T(8,128)(2,1)S(1)} async-done(((bf16[16,6,128,128]{3,2,1,0:T(8,128)(2,1)}), bf16[16,6,128,128]{3,2,1,0:T(8,128)(2,1)S(1)}, u32[]{:S(2)}, u32[]{:S(2)}) %all-to-all-start.1) | async-done | bytes 3145760 | tf_op jit(solution)/shard_map/all_to_all | solution.py:72
  300.3 2.7 gather_fusion.2
  303.0 3.4 %fusion.1 = bf16[1,1,96,128,128]{4,3,2,1,0:T(8,128)(2,1)} fusion(bf16[96,128,128]{2,1,0:T(8,128)(2,1)} %gather_fusion.2, pred[96]{0:T(512)(128)(4,1)S(1)} %get-tuple-element.8, pred[96]{0:T(512)(128)(4,1)S(1)} %get-tuple-element.9), kind=kLoop, calls=%fused_computation.8 | loop fusion | flops 3145728 | bytes 6291648 | tf_op jit(solution)/shard_map/jit(_where)/select_n | solution.py:21
  (34 shorter events, 2.5 us)
Async XLA Ops:
  7.2 5.9 %copy-start = (s32[16,16]{1,0:T(8,128)S(1)}, s32[16,16]{1,0:T(8,128)}, u32[]{:S(2)}) copy-start(s32[16,16]{1,0:T(8,128)} %param.4) | copy-start | bytes 3076
  7.2 116.8 %all-gather.3.cloned.1.call-start = ((), (), s32[]{:S(2)}) async-start(), calls=%async_computation.2 | async-start | bytes 3481600 | tf_op jit(solution)/shard_map/all_gather | solution.py:32
  11.3 174.2 %all-gather.5.cloned.1.call-start = ((), (), s32[]{:S(2)}) async-start(), calls=%async_computation.3 | async-start | bytes 3481600 | tf_op jit(solution)/shard_map/all_gather | solution.py:35
  15.1 209.8 %all-to-all-start = ((s32[16,1,6]{2,1,0:T(1,128)}), s32[16,1,6]{2,1,0:T(1,128)S(1)}, u32[]{:S(2)}, u32[]{:S(2)}) async-start(s32[16,1,6]{2,1,0:T(1,128)} %copy.18), calls=%async_computation | async-start | bytes 16384 | tf_op jit(solution)/shard_map/all_to_all | solution.py:73
  224.9 75.4 %all-to-all-start.1 = ((bf16[16,6,128,128]{3,2,1,0:T(8,128)(2,1)}), bf16[16,6,128,128]{3,2,1,0:T(8,128)(2,1)S(1)}, u32[]{:S(2)}, u32[]{:S(2)}) async-start(bf16[16,6,128,128]{3,2,1,0:T(8,128)(2,1)} %broadcast_select_fusion), calls=%async_computation.1 | async-start | bytes 6291456 | tf_op jit(solution)/shard_map/all_to_all | solution.py:72
Sparse Core Ops, SparseCore 0:
  11.4 112.5 all-gather.2
  126.6 58.8 all-gather.4
where the time goes:
time: 314 us; the launch traced here: 313 us
  waiting for transfers between devices  192 us (61%)
  starting transfers between devices  49.2 us (16%)
  local copies, waits for them, and re-layouts  31.4 us (10%)
  between operations  14.2 us (5%)
  matrix products  13.6 us (4%)
  other arithmetic  13.2 us (4%)
    all_to_all x1, waiting for transfers between devices, shards(): lax.all_to_all(outgoing, 'row', split_axis=0, concat_axis=0, tiled=True)  65.3 us
    all_gather x1, waiting for transfers between devices, shards(): row_block = lax.all_gather(scored, 'col', axis=1, tiled=True)  64 us
    all_gather x1, waiting for transfers between devices, shards(): lax.all_gather(scored, 'row', axis=1, tiled=True)  61.5 us
    all_to_all x1, starting transfers between devices, shards(): lax.all_to_all(out_ids, 'row', split_axis=0, concat_axis=0, tiled=True)  44.6 us
    dot_general x1, matrix products, shards(): lax.dot_general(row_block, lax.all_gather(scored, 'row', axis=1, tiled=Tr...  13.6 us
    unnamed x3, local copies, waits for them, and re-layouts  9.76 us
    reshape x1, local copies, waits for them, and re-layouts, shards(): tile_grid.reshape(row_count, TILE, col_count, TILE).transpose(0, 2, 1, 3)  9.11 us
  transfers between devices with their start and end apart: 4, of which 3 were waited for; matrix products, arithmetic and copies ran while one was open for 15% of the time, Pallas kernels for 0%

commit v1 on v0

v1 whole, which is shorter than its diff:
```python
import functools

import jax
import jax.numpy as jnp
from jax import lax
from jax.experimental import pallas as pl
from jax.experimental.pallas import tpu as pltpu
from jax.sharding import PartitionSpec as P

EPS = 1e-05
LANES = 128
ALIGN = 8
COPIES = 2
VMEM_LIMIT = 24 * 2**20

VMEM = pl.BlockSpec(memory_space=pltpu.VMEM)
SMEM = pl.BlockSpec(memory_space=pltpu.SMEM)


def score_kernel(series_ref, scored_ref, chunks_ref):
    frames = series_ref.shape[0]
    _, sub, padded = chunks_ref.shape
    groups = LANES // sub
    x = series_ref[...]
    centred = x - jnp.sum(x, axis=0, keepdims=True) * (1.0 / frames)
    spread = jnp.sum(centred * centred, axis=0, keepdims=True) * (1.0 / frames)
    z = centred * lax.rsqrt(spread + EPS)
    scored_ref[...] = z.astype(jnp.bfloat16)
    for b in range(padded // LANES):
        rows = min(LANES, frames - b * LANES)
        part = z[b * LANES : b * LANES + rows]
        if rows < LANES:
            part = jnp.concatenate([part, jnp.zeros((LANES - rows, LANES), jnp.float32)], axis=0)
        flipped = part.T.astype(jnp.bfloat16)
        flipped = flipped.reshape(groups, sub, LANES)
        for copy in range(COPIES):
            at = copy * groups
            chunks_ref[at : at + groups, :, b * LANES : (b + 1) * LANES] = flipped


def route_kernel(frames, where_ref, owner_ref, chunks_ref, keep_ref, out_ref):
    n = chunks_ref.shape[0]
    padded = chunks_ref.shape[2]
    last = padded - LANES
    gap = frames - last
    flags = keep_ref[...].astype(jnp.float32)
    flags = jnp.concatenate(
        [
            jnp.zeros((n, gap), jnp.float32),
            flags,
            jnp.zeros((n, LANES - gap - flags.shape[1]), jnp.float32),
        ],
        axis=1,
    )
    base = where_ref[0] * n
    for k in range(n):
        owner = owner_ref[base + k]
        out_ref[owner, :, :last] = chunks_ref[k, :, :last]
        tail = chunks_ref[k, :, last:].astype(jnp.float32) + flags[k : k + 1]
        out_ref[owner, :, last:] = tail.astype(jnp.bfloat16)


def pack_kernel(frames, where_ref, got_ref, owner_ref, packed_ref, code_ref, ids_ref):
    n, sub, padded = got_ref.shape
    rows = n * sub
    last = padded - LANES
    gap = frames - last
    for b in range(last // LANES):
        block = got_ref[:, :, b * LANES : (b + 1) * LANES]
        packed_ref[b * rows : (b + 1) * rows, :] = block.reshape(rows, LANES)
    tail = got_ref[:, :, last:].reshape(rows, LANES)
    per = LANES // gap
    depth = rows // per
    packed_ref[last // LANES * rows :, :] = jnp.concatenate(
        [tail[q * depth : (q + 1) * depth, :gap] for q in range(per)], axis=1
    )
    me = where_ref[0]
    block = where_ref[1]
    flags = got_ref[:, 0, last:].astype(jnp.float32)[:, gap : gap + n]
    r_of = lax.broadcasted_iota(jnp.int32, (n, n), 0)
    k_of = lax.broadcasted_iota(jnp.int32, (n, n), 1)
    upper = (r_of <= k_of).astype(jnp.float32)
    lower = (r_of > k_of).astype(jnp.float32)
    within = jnp.dot(flags, upper, preferred_element_type=jnp.float32)
    before = jnp.sum(
        jnp.dot(lower, flags, preferred_element_type=jnp.float32), axis=1, keepdims=True
    )
    place = (before + within - 1.0).astype(jnp.int32)
    place = jnp.where(flags > 0.5, place, -1)
    picked = jnp.sum(jnp.where(owner_ref[...] == me, k_of, 0), axis=1, keepdims=True)
    lane = lax.broadcasted_iota(jnp.int32, (n, LANES), 1)
    row = lax.broadcasted_iota(jnp.int32, (n, LANES), 0)
    tiles = n * n
    found = jnp.zeros((n, LANES), jnp.int32)
    code = jnp.zeros((n, LANES), jnp.int32)
    ids = jnp.zeros((n, LANES), jnp.int32)
    for j in range(n):
        hit = place[:, j : j + 1] == lane
        found = found + hit.astype(jnp.int32)
        code = code + jnp.where(hit, j * rows + row * sub, 0)
        ids = ids + jnp.where(hit, (row * n + picked) * tiles + block * n + j, 0)
    found = jnp.sum(found, axis=0, keepdims=True)
    code = jnp.where(found > 0, jnp.sum(code, axis=0, keepdims=True), n * rows)
    ids = jnp.where(found > 0, jnp.sum(ids, axis=0, keepdims=True), -1)
    code_ref[...] = jnp.broadcast_to(code, code_ref.shape)
    ids_ref[0] = ids[:, : ids_ref.shape[2]]


def strip_kernel(scale, frames, offset, where_ref, code_ref, part, cols_ref, _, out_ref, prod_ref):
    n = cols_ref.shape[0]
    slots = out_ref.shape[0]
    rows = prod_ref.shape[0] // (n + 1)
    sub = rows // n
    groups = LANES // sub
    last = frames // LANES
    gap = frames - last * LANES
    pieces = [part[b * rows : (b + 1) * rows, :] for b in range(last)]
    tail = part[last * rows :, :]
    pieces.append(jnp.concatenate([tail[:, q : q + gap] for q in range(0, LANES, gap)], axis=0))
    left = jnp.concatenate(pieces, axis=1)
    prod_ref[n * rows : n * rows + sub, :] = jnp.zeros((sub, LANES), jnp.float32)
    for g in range(n // 2):
        pair = jnp.concatenate([cols_ref[2 * g], cols_ref[2 * g + 1]], axis=1)
        prod = jnp.dot(left, pair, preferred_element_type=jnp.float32)
        for h in range(2):
            at = (2 * g + h) * rows
            prod_ref[at : at + rows, :] = prod[:, h * LANES : (h + 1) * LANES]
    group = lax.rem(where_ref[1] + (offset + groups), groups)
    into = pl.ds(pl.multiple_of(group * sub, sub), sub)
    for s in range(slots):
        strip = prod_ref[pl.ds(pl.multiple_of(code_ref[0, s], sub), sub), :]
        out_ref[s, into, :] = (strip * scale).astype(jnp.bfloat16)


def in_vmem(x):
    return pltpu.with_memory_space_constraint(x, pltpu.VMEM)


def strips(part, offset, where, code, cols, out, scale):
    n, frames, _ = cols.shape
    rows = part.shape[0] * LANES // frames
    return pl.pallas_call(
        functools.partial(strip_kernel, scale, frames, offset),
        out_shape=pltpu.VMEM(out.shape, out.dtype),
        in_specs=[SMEM, SMEM, VMEM, VMEM, VMEM],
        out_specs=VMEM,
        input_output_aliases={4: 0},
        scratch_shapes=[pltpu.VMEM(((n + 1) * rows, LANES), jnp.float32)],
        compiler_params=pltpu.CompilerParams(vmem_limit_bytes=VMEM_LIMIT),
        name="strips",
    )(where, code, in_vmem(part), in_vmem(cols), in_vmem(out))


def alloc(shape, dtype):
    def nothing(out_ref):
        pass

    return pl.pallas_call(
        nothing,
        out_shape=pltpu.VMEM(shape, dtype),
        out_specs=VMEM,
        compiler_params=pltpu.CompilerParams(vmem_limit_bytes=VMEM_LIMIT),
        name="alloc",
    )()


def shards(series, keep_mask, row_owner):
    frames = series.shape[0]
    n_row = lax.axis_size("row")
    n_col = lax.axis_size("col")
    row_count, col_count = keep_mask.shape
    slot_limit = max(2, 3 * col_count // 8)
    capacity = row_count * slot_limit
    padded = -(-frames // LANES) * LANES
    groups = n_col // COPIES
    sub = LANES // groups
    my_row = lax.axis_index("row")
    my_col = lax.axis_index("col")
    where = jnp.stack([my_row, my_col]).astype(jnp.int32)
    bf16 = jnp.bfloat16
    sds = jax.ShapeDtypeStruct

    scored, chunks = pl.pallas_call(
        score_kernel,
        out_shape=(sds((frames, LANES), bf16), sds((n_col, sub, padded), bf16)),
        in_specs=[VMEM],
        out_specs=(VMEM, VMEM),
        name="score",
    )(series)

    mixed = lax.all_to_all(chunks, "col", 0, 0, tiled=True)
    routed = pl.pallas_call(
        functools.partial(route_kernel, frames),
        out_shape=sds((n_row, sub, padded), bf16),
        in_specs=[SMEM, SMEM, VMEM, VMEM],
        out_specs=VMEM,
        name="route",
    )(where, row_owner, mixed, keep_mask)
    got = lax.all_to_all(routed, "row", 0, 0, tiled=True)
    packed, code, ids = pl.pallas_call(
        functools.partial(pack_kernel, frames),
        out_shape=(
            sds((frames * n_row * sub // LANES, LANES), bf16),
            sds((ALIGN, LANES), jnp.int32),
            sds((1, 1, capacity), jnp.int32),
        ),
        in_specs=[SMEM, VMEM, VMEM],
        out_specs=(VMEM, VMEM, VMEM),
        name="pack",
    )(where, got, row_owner.reshape(n_row, row_count))

    cols = lax.all_gather(scored, "row", axis=0, tiled=False)

    out = alloc((capacity, LANES, LANES), bf16)
    cols = in_vmem(cols)
    fill = functools.partial(strips, where=where, code=code, cols=cols, scale=1.0 / frames)
    right = [(i, (i + 1) % n_col) for i in range(n_col)]
    left = [(i, (i - 1) % n_col) for i in range(n_col)]
    half = groups // 2
    a = lax.ppermute(packed, "col", right)
    b = lax.ppermute(packed, "col", left)
    out = fill(packed, 0, out=out)
    for step in range(1, half + 1):
        here, there = a, b
        if step < half:
            here, out = lax.optimization_barrier((here, out))
            a = lax.ppermute(here, "col", right)
        out = fill(here, -step, out=out)
        if step < half:
            if step < half - 1:
                there, out = lax.optimization_barrier((there, out))
                b = lax.ppermute(there, "col", left)
            out = fill(there, step, out=out)
    return out.reshape(1, 1, capacity, LANES, LANES), ids


def solution(mesh):
    in_specs = (P(None, ("subj", "row", "col")), P(("subj", "row"), "col"), P("subj"))
    out_specs = (P(("subj", "row"), "col", None, None, None), P(("subj", "row"), "col", None))
    return jax.shard_map(shards, mesh=mesh, in_specs=in_specs, out_specs=out_specs, check_vma=False)
```

time: 314 us -> 178 us (0.57)
  waiting for transfers between devices: 192 us -> 50.1 us
  starting transfers between devices: 49.2 us -> 81.1 us
  local copies, waits for them, and re-layouts: 31.4 us -> 7.06 us
  Pallas kernels: 0 us -> 22.8 us
  matrix products: 13.6 us -> 0 us
  other arithmetic: 13.2 us -> 0.56 us
    all_gather x2 -> x1, waiting for transfers between devices: 125 us -> 0.02 us  [shards(): cols = lax.all_gather(scored, 'row', axis=0, tiled=False)]
    all_to_all x2, waiting for transfers between devices: 65.3 us -> 35.2 us  [the longest x1 20.1 us: shards(): mixed = lax.all_to_all(chunks, 'col', 0, 0, tiled=True)]
    pallas_call x0 -> x12, Pallas kernels: none -> 22.8 us  [the longest x8 16.5 us: strips(): pl.pallas_call(functools.partial(strip_kernel, scale, frames, offset), ou...]
    ppermute x0 -> x7, starting transfers between devices: none -> 22.4 us  [the longest x2 9.21 us: shards(): b = lax.ppermute(there, 'col', left)]
    ppermute x0 -> x7, waiting for transfers between devices: none -> 14.8 us  [the longest x3 13.2 us: shards(): a = lax.ppermute(here, 'col', right)]
    dot_general x1 -> x0, matrix products: 13.6 us -> none  [shards(): lax.dot_general(row_block, lax.all_gather(scored, 'row', axis=1, tiled=Tr...]
    all_to_all x2, starting transfers between devices: 49.1 us -> 58.6 us  [the longest x1 44.2 us: shards(): mixed = lax.all_to_all(chunks, 'col', 0, 0, tiled=True)]
    gather x4 -> x0, local copies, waits for them, and re-layouts: 9.43 us -> none  [the longest x1 4.92 us: shards(): chosen = tile_grid[row_of[:, None], picked]]
  transfers between devices with their start and end apart: 4 -> 10, of which waited for: 3 -> 6; matrix products, arithmetic and copies ran while one was open for 15% -> 1% of each run, Pallas kernels for 0% -> 11%
where the time goes in v1:
time: 178 us; the launch traced here: 176 us
  starting transfers between devices  81.1 us (46%)
  waiting for transfers between devices  50.1 us (28%)
  Pallas kernels  22.8 us (13%)
  between operations  14.3 us (8%)
  local copies, waits for them, and re-layouts  7.06 us (4%)
    all_to_all x1, starting transfers between devices, shards(): mixed = lax.all_to_all(chunks, 'col', 0, 0, tiled=True)  44.2 us
    all_to_all x1, waiting for transfers between devices, shards(): mixed = lax.all_to_all(chunks, 'col', 0, 0, tiled=True)  20.1 us
    pallas_call x8, Pallas kernels, strips(): pl.pallas_call(functools.partial(strip_kernel, scale, frames, offset), ou...  16.5 us
    all_to_all x1, waiting for transfers between devices, shards(): got = lax.all_to_all(routed, 'row', 0, 0, tiled=True)  15.2 us
    all_to_all x1, starting transfers between devices, shards(): got = lax.all_to_all(routed, 'row', 0, 0, tiled=True)  14.4 us
    ppermute x3, waiting for transfers between devices, shards(): a = lax.ppermute(here, 'col', right)  13.2 us
    ppermute x2, starting transfers between devices, shards(): b = lax.ppermute(there, 'col', left)  9.21 us
    unnamed x17, local copies, waits for them, and re-layouts  6.39 us
  transfers between devices with their start and end apart: 10, of which 6 were waited for; matrix products, arithmetic and copies ran while one was open for 1% of the time, Pallas kernels for 11%

profile of v1, /device:TPU:65, one launch (start us, length us, event | category | flops | bytes accessed | tf_op | source)
XLA Modules:
  0.0 175.9 jit_solution(1782044052016501565)
XLA Ops:
  7.3 2.1 %score.1 = (bf16[800,128]{1,0:T(8,128)(2,1)}, bf16[16,16,896]{2,1,0:T(8,128)(2,1)}) custom-call(f32[800,128]{1,0:T(8,128)} %series_ref.1), custom_call_target="tpu_custom_call" | custom-call | tf_op jit(solution)/shard_map/score/pallas_call | solution.py:183
  9.5 44.2 %all-to-all-start = ((bf16[16,16,896]{2,1,0:T(8,128)(2,1)}), bf16[16,16,896]{2,1,0:T(8,128)(2,1)S(1)}, u32[]{:S(2)}, u32[]{:S(2)}) async-start(bf16[16,16,896]{2,1,0:T(8,128)(2,1)} %get-tuple-element.17), calls=%async_computation | async-start | bytes 917504 | tf_op jit(solution)/shard_map/all_to_all | solution.py:191
  54.3 20.1 %all-to-all-done.chunks_ref = bf16[16,16,896]{2,1,0:T(8,128)(2,1)S(1)} async-done(((bf16[16,16,896]{2,1,0:T(8,128)(2,1)}), bf16[16,16,896]{2,1,0:T(8,128)(2,1)S(1)}, u32[]{:S(2)}, u32[]{:S(2)}) %all-to-all-start) | async-done | bytes 458784 | tf_op jit(solution)/shard_map/all_to_all | solution.py:191
  77.0 14.4 %all-to-all-start.1 = ((bf16[16,16,896]{2,1,0:T(8,128)(2,1)}), bf16[16,16,896]{2,1,0:T(8,128)(2,1)S(1)}, u32[]{:S(2)}, u32[]{:S(2)}) async-start(bf16[16,16,896]{2,1,0:T(8,128)(2,1)} %route.1), calls=%async_computation.1 | async-start | bytes 917504 | tf_op jit(solution)/shard_map/all_to_all | solution.py:199
  92.1 15.2 %all-to-all-done.1.got_ref = bf16[16,16,896]{2,1,0:T(8,128)(2,1)S(1)} async-done(((bf16[16,16,896]{2,1,0:T(8,128)(2,1)}), bf16[16,16,896]{2,1,0:T(8,128)(2,1)S(1)}, u32[]{:S(2)}, u32[]{:S(2)}) %all-to-all-start.1) | async-done | bytes 458784 | tf_op jit(solution)/shard_map/all_to_all | solution.py:199
  108.0 2.2 %pack.1 = (bf16[1600,128]{1,0:T(8,128)(2,1)}, s32[8,128]{1,0:T(8,128)}, s32[1,1,96]{2,1,0:T(1,128)}) custom-call(s32[2]{0:T(128)} %pad_add_fusion.where_ref, bf16[16,16,896]{2,1,0:T(8,128)(2,1)} %copy-done.6, s32[16,16]{1,0:T(8,128)} %reshape.10.owner_ref), custom_call_target="tpu_custom_call" | custom-call | tf_op jit(solution)/shard_map/pack/pallas_call | solution.py:200
  110.2 1.9 %collective-permute-start = (bf16[1600,128]{1,0:T(8,128)(2,1)}, bf16[1600,128]{1,0:T(8,128)(2,1)}, u32[]{:S(2)}, u32[]{:S(2)}) collective-permute-start(bf16[1600,128]{1,0:T(8,128)(2,1)} %get-tuple-element.19.part), channel_id=1, source_target_pairs={{0,1},{1,2},{2,3},{3,4},{4,5},{5,6},{6,7},{7,8},{8,9},{9,10},{10,1... | collective-permute-start | bytes 1228808 | tf_op jit(solution)/shard_map/ppermute | solution.py:220
  112.2 5.5 %collective-permute-start.2 = (bf16[1600,128]{1,0:T(8,128)(2,1)}, bf16[1600,128]{1,0:T(8,128)(2,1)S(1)}, u32[]{:S(2)}, u32[]{:S(2)}) collective-permute-start(bf16[1600,128]{1,0:T(8,128)(2,1)} %get-tuple-element.19.part), channel_id=1, source_target_pairs={{0,15},{1,0},{2,1},{3,2},{4,3},{5,4},{6,5},{7,6},{8,7},{9,8},{10,9... | collective-permute-start | bytes 1228808 | tf_op jit(solution)/shard_map/ppermute | solution.py:221
  120.9 2.5 %strips.8._ = bf16[96,128,128]{2,1,0:T(8,128)(2,1)S(1)} custom-call(s32[2]{0:T(128)S(1)} %copy-done.4, s32[8,128]{1,0:T(8,128)S(1)} %copy-done.2, bf16[1600,128]{1,0:T(8,128)(2,1)} %get-tuple-element.19.part, bf16[16,800,128]{2,1,0:T(8,128)(2,1)S(1)} %bitcast.5, bf16[96,128,128]{2,1,0:T(8,128)(2,1)S(1)} %alloc.1._), custom_call_target="tpu_custom_call", output_to_operand_aliasing={{}: (4, {})} | custom-call | tf_op jit(solution)/shard_map/strips/pallas_call | solution.py:142
  124.9 1.9 %collective-permute-start.1 = (bf16[1600,128]{1,0:T(8,128)(2,1)}, bf16[1600,128]{1,0:T(8,128)(2,1)S(1)}, u32[]{:S(2)}, u32[]{:S(2)}) collective-permute-start(bf16[1600,128]{1,0:T(8,128)(2,1)} %collective-permute-done.part), channel_id=1, source_target_pairs={{0,1},{1,2},{2,3},{3,4},{4,5},{5,6},{6,7},{7,8},{8,9},{9,10},{10,1... | collective-permute-start | bytes 1228808 | tf_op jit(solution)/shard_map/ppermute | solution.py:227
  126.9 2.4 %strips.9._ = bf16[96,128,128]{2,1,0:T(8,128)(2,1)S(1)} custom-call(s32[2]{0:T(128)S(1)} %copy-done.4, s32[8,128]{1,0:T(8,128)S(1)} %copy-done.3, bf16[1600,128]{1,0:T(8,128)(2,1)} %collective-permute-done.part, bf16[16,800,128]{2,1,0:T(8,128)(2,1)S(1)} %bitcast.6, bf16[96,128,128]{2,1,0:T(8,128)(2,1)S(1)} %strips.8._), custom_call_target="tpu_custom_call", output_to_operand_aliasing={{}: (4, {})} | custom-call | tf_op jit(solution)/shard_map/strips/pallas_call | solution.py:142
  129.3 4.6 %collective-permute-start.4 = (bf16[1600,128]{1,0:T(8,128)(2,1)S(1)}, bf16[1600,128]{1,0:T(8,128)(2,1)S(1)}, u32[]{:S(2)}, u32[]{:S(2)}) collective-permute-start(bf16[1600,128]{1,0:T(8,128)(2,1)S(1)} %collective-permute-done.2.part), channel_id=1, source_target_pairs={{0,15},{1,0},{2,1},{3,2},{4,3},{5,4},{6,5},{7,6},{8,7},{9,8},{10,9... | collective-permute-start | bytes 1228808 | tf_op jit(solution)/shard_map/ppermute | solution.py:232
  133.9 1.9 %strips.10._ = bf16[96,128,128]{2,1,0:T(8,128)(2,1)S(1)} custom-call(s32[2]{0:T(128)S(1)} %copy-done.4, s32[8,128]{1,0:T(8,128)S(1)} %copy-done.3, bf16[1600,128]{1,0:T(8,128)(2,1)S(1)} %collective-permute-done.2.part, bf16[16,800,128]{2,1,0:T(8,128)(2,1)S(1)} %bitcast.7, bf16[96,128,128]{2,1,0:T(8,128)(2,1)S(1)} %strips.9._), custom_call_target="tpu_custom_call", output_to_operand_aliasing={{}: (4, {})} | custom-call | tf_op jit(solution)/shard_map/strips/pallas_call | solution.py:142
  135.8 3.6 %collective-permute-done.1.part = bf16[1600,128]{1,0:T(8,128)(2,1)S(1)} collective-permute-done((bf16[1600,128]{1,0:T(8,128)(2,1)}, bf16[1600,128]{1,0:T(8,128)(2,1)S(1)}, u32[]{:S(2)}, u32[]{:S(2)}) %collective-permute-start.1) | collective-permute-done | bytes 409632 | tf_op jit(solution)/shard_map/ppermute | solution.py:227
  139.4 1.9 %collective-permute-start.3 = (bf16[1600,128]{1,0:T(8,128)(2,1)S(1)}, bf16[1600,128]{1,0:T(8,128)(2,1)S(1)}, u32[]{:S(2)}, u32[]{:S(2)}) collective-permute-start(bf16[1600,128]{1,0:T(8,128)(2,1)S(1)} %collective-permute-done.1.part), channel_id=1, source_target_pairs={{0,1},{1,2},{2,3},{3,4},{4,5},{5,6},{6,7},{7,8},{8,9},{9,10},{10,1... | collective-permute-start | bytes 1228808 | tf_op jit(solution)/shard_map/ppermute | solution.py:227
  141.4 1.9 %strips.11._ = bf16[96,128,128]{2,1,0:T(8,128)(2,1)S(1)} custom-call(s32[2]{0:T(128)S(1)} %copy-done.4, s32[8,128]{1,0:T(8,128)S(1)} %copy-done.3, bf16[1600,128]{1,0:T(8,128)(2,1)S(1)} %collective-permute-done.1.part, bf16[16,800,128]{2,1,0:T(8,128)(2,1)S(1)} %bitcast.8, bf16[96,128,128]{2,1,0:T(8,128)(2,1)S(1)} %strips.10._), custom_call_target="tpu_custom_call", output_to_operand_aliasing={{}: (4, {})} | custom-call | tf_op jit(solution)/shard_map/strips/pallas_call | solution.py:142
  143.3 4.6 %collective-permute-start.6 = (bf16[1600,128]{1,0:T(8,128)(2,1)S(1)}, bf16[1600,128]{1,0:T(8,128)(2,1)S(1)}, u32[]{:S(2)}, u32[]{:S(2)}) collective-permute-start(bf16[1600,128]{1,0:T(8,128)(2,1)S(1)} %collective-permute-done.4.part), channel_id=1, source_target_pairs={{0,15},{1,0},{2,1},{3,2},{4,3},{5,4},{6,5},{7,6},{8,7},{9,8},{10,9... | collective-permute-start | bytes 1228808 | tf_op jit(solution)/shard_map/ppermute | solution.py:232
  147.9 1.9 %strips.12._ = bf16[96,128,128]{2,1,0:T(8,128)(2,1)S(1)} custom-call(s32[2]{0:T(128)S(1)} %copy-done.4, s32[8,128]{1,0:T(8,128)S(1)} %copy-done.3, bf16[1600,128]{1,0:T(8,128)(2,1)S(1)} %collective-permute-done.4.part, bf16[16,800,128]{2,1,0:T(8,128)(2,1)S(1)} %bitcast.9, bf16[96,128,128]{2,1,0:T(8,128)(2,1)S(1)} %strips.11._), custom_call_target="tpu_custom_call", output_to_operand_aliasing={{}: (4, {})} | custom-call | tf_op jit(solution)/shard_map/strips/pallas_call | solution.py:142
  149.9 2.9 %collective-permute-done.3.part = bf16[1600,128]{1,0:T(8,128)(2,1)S(1)} collective-permute-done((bf16[1600,128]{1,0:T(8,128)(2,1)S(1)}, bf16[1600,128]{1,0:T(8,128)(2,1)S(1)}, u32[]{:S(2)}, u32[]{:S(2)}) %collective-permute-start.3) | collective-permute-done | bytes 409632 | tf_op jit(solution)/shard_map/ppermute | solution.py:227
  152.8 1.9 %collective-permute-start.5 = (bf16[1600,128]{1,0:T(8,128)(2,1)S(1)}, bf16[1600,128]{1,0:T(8,128)(2,1)S(1)}, u32[]{:S(2)}, u32[]{:S(2)}) collective-permute-start(bf16[1600,128]{1,0:T(8,128)(2,1)S(1)} %collective-permute-done.3.part), channel_id=1, source_target_pairs={{0,1},{1,2},{2,3},{3,4},{4,5},{5,6},{6,7},{7,8},{8,9},{9,10},{10,1... | collective-permute-start | bytes 1228808 | tf_op jit(solution)/shard_map/ppermute | solution.py:227
  154.8 1.9 %strips.13._ = bf16[96,128,128]{2,1,0:T(8,128)(2,1)S(1)} custom-call(s32[2]{0:T(128)S(1)} %copy-done.4, s32[8,128]{1,0:T(8,128)S(1)} %copy-done.3, bf16[1600,128]{1,0:T(8,128)(2,1)S(1)} %collective-permute-done.3.part, bf16[16,800,128]{2,1,0:T(8,128)(2,1)S(1)} %bitcast.10, bf16[96,128,128]{2,1,0:T(8,128)(2,1)S(1)} %strips.12._), custom_call_target="tpu_custom_call", output_to_operand_aliasing={{}: (4, {})} | custom-call | tf_op jit(solution)/shard_map/strips/pallas_call | solution.py:142
  156.7 1.9 %strips.14._ = bf16[96,128,128]{2,1,0:T(8,128)(2,1)S(1)} custom-call(s32[2]{0:T(128)S(1)} %copy-done.4, s32[8,128]{1,0:T(8,128)S(1)} %copy-done.3, bf16[1600,128]{1,0:T(8,128)(2,1)S(1)} %collective-permute-done.6.part, bf16[16,800,128]{2,1,0:T(8,128)(2,1)S(1)} %bitcast.11, bf16[96,128,128]{2,1,0:T(8,128)(2,1)S(1)} %strips.13._), custom_call_target="tpu_custom_call", output_to_operand_aliasing={{}: (4, {})} | custom-call | tf_op jit(solution)/shard_map/strips/pallas_call | solution.py:142
  158.7 6.7 %collective-permute-done.5.part = bf16[1600,128]{1,0:T(8,128)(2,1)S(1)} collective-permute-done((bf16[1600,128]{1,0:T(8,128)(2,1)S(1)}, bf16[1600,128]{1,0:T(8,128)(2,1)S(1)}, u32[]{:S(2)}, u32[]{:S(2)}) %collective-permute-start.5) | collective-permute-done | bytes 409632 | tf_op jit(solution)/shard_map/ppermute | solution.py:227
  165.4 1.9 %strips.15 = bf16[96,128,128]{2,1,0:T(8,128)(2,1)S(1)} custom-call(s32[2]{0:T(128)S(1)} %copy-done.4, s32[8,128]{1,0:T(8,128)S(1)} %copy-done.3, bf16[1600,128]{1,0:T(8,128)(2,1)S(1)} %collective-permute-done.5.part, bf16[16,800,128]{2,1,0:T(8,128)(2,1)S(1)} %bitcast.12, bf16[96,128,128]{2,1,0:T(8,128)(2,1)S(1)} %strips.14._), custom_call_target="tpu_custom_call", output_to_operand_aliasing={{}: (4, {})} | custom-call | tf_op jit(solution)/shard_map/strips/pallas_call | solution.py:142
  (28 shorter events, 11.2 us)
Async XLA Ops:
  7.2 84.2 %copy-start.7 = (s32[256]{0:T(256)S(1)}, s32[256]{0:T(256)}, u32[]{:S(2)}) copy-start(s32[256]{0:T(256)} %owner_ref.1) | copy-start | bytes 3076
  7.2 110.5 %all-gather.3.cloned.1.call-start = ((), (), s32[]{:S(2)}) async-start(), calls=%async_computation.2 | async-start | bytes 3481600 | tf_op jit(solution)/shard_map/all_gather | solution.py:212
  9.5 64.9 %all-to-all-start = ((bf16[16,16,896]{2,1,0:T(8,128)(2,1)}), bf16[16,16,896]{2,1,0:T(8,128)(2,1)S(1)}, u32[]{:S(2)}, u32[]{:S(2)}) async-start(bf16[16,16,896]{2,1,0:T(8,128)(2,1)} %get-tuple-element.17), calls=%async_computation | async-start | bytes 917504 | tf_op jit(solution)/shard_map/all_to_all | solution.py:191
  74.3 0.8 copy-start.5
  77.0 30.3 %all-to-all-start.1 = ((bf16[16,16,896]{2,1,0:T(8,128)(2,1)}), bf16[16,16,896]{2,1,0:T(8,128)(2,1)S(1)}, u32[]{:S(2)}, u32[]{:S(2)}) async-start(bf16[16,16,896]{2,1,0:T(8,128)(2,1)} %route.1), calls=%async_computation.1 | async-start | bytes 917504 | tf_op jit(solution)/shard_map/all_to_all | solution.py:199
  107.3 0.8 copy-start.6
  110.2 14.7 %collective-permute-start = (bf16[1600,128]{1,0:T(8,128)(2,1)}, bf16[1600,128]{1,0:T(8,128)(2,1)}, u32[]{:S(2)}, u32[]{:S(2)}) collective-permute-start(bf16[1600,128]{1,0:T(8,128)(2,1)} %get-tuple-element.19.part), channel_id=1, source_target_pairs={{0,1},{1,2},{2,3},{3,4},{4,5},{5,6},{6,7},{7,8},{8,9},{9,10},{10,1... | collective-permute-start | bytes 1228808 | tf_op jit(solution)/shard_map/ppermute | solution.py:220
  112.2 17.1 %collective-permute-start.2 = (bf16[1600,128]{1,0:T(8,128)(2,1)}, bf16[1600,128]{1,0:T(8,128)(2,1)S(1)}, u32[]{:S(2)}, u32[]{:S(2)}) collective-permute-start(bf16[1600,128]{1,0:T(8,128)(2,1)} %get-tuple-element.19.part), channel_id=1, source_target_pairs={{0,15},{1,0},{2,1},{3,2},{4,3},{5,4},{6,5},{7,6},{8,7},{9,8},{10,9... | collective-permute-start | bytes 1228808 | tf_op jit(solution)/shard_map/ppermute | solution.py:221
  117.7 1.9 %copy-start = (bf16[12800,128]{1,0:T(8,128)(2,1)S(1)}, bf16[12800,128]{1,0:T(8,128)(2,1)}, u32[]{:S(2)}) copy-start(bf16[12800,128]{1,0:T(8,128)(2,1)} %all-gather.3.cloned.1.call-done) | copy-start | bytes 9830404
  119.6 0.7 copy-start.2
  120.3 0.6 copy-start.4
  120.9 6.0 %copy-start.1 = (bf16[12800,128]{1,0:T(8,128)(2,1)S(1)}, bf16[12800,128]{1,0:T(8,128)(2,1)}, u32[]{:S(2)}) copy-start(bf16[12800,128]{1,0:T(8,128)(2,1)} %all-gather.3.cloned.1.call-done) | copy-start | bytes 9830404
  120.9 6.0 %copy-start.3 = (s32[8,128]{1,0:T(8,128)S(1)}, s32[8,128]{1,0:T(8,128)}, u32[]{:S(2)}) copy-start(s32[8,128]{1,0:T(8,128)} %get-tuple-element.18.code_ref) | copy-start | bytes 12292
  124.9 14.5 %collective-permute-start.1 = (bf16[1600,128]{1,0:T(8,128)(2,1)}, bf16[1600,128]{1,0:T(8,128)(2,1)S(1)}, u32[]{:S(2)}, u32[]{:S(2)}) collective-permute-start(bf16[1600,128]{1,0:T(8,128)(2,1)} %collective-permute-done.part), channel_id=1, source_target_pairs={{0,1},{1,2},{2,3},{3,4},{4,5},{5,6},{6,7},{7,8},{8,9},{9,10},{10,1... | collective-permute-start | bytes 1228808 | tf_op jit(solution)/shard_map/ppermute | solution.py:227
  129.3 14.0 %collective-permute-start.4 = (bf16[1600,128]{1,0:T(8,128)(2,1)S(1)}, bf16[1600,128]{1,0:T(8,128)(2,1)S(1)}, u32[]{:S(2)}, u32[]{:S(2)}) collective-permute-start(bf16[1600,128]{1,0:T(8,128)(2,1)S(1)} %collective-permute-done.2.part), channel_id=1, source_target_pairs={{0,15},{1,0},{2,1},{3,2},{4,3},{5,4},{6,5},{7,6},{8,7},{9,8},{10,9... | collective-permute-start | bytes 1228808 | tf_op jit(solution)/shard_map/ppermute | solution.py:232
  139.4 13.4 %collective-permute-start.3 = (bf16[1600,128]{1,0:T(8,128)(2,1)S(1)}, bf16[1600,128]{1,0:T(8,128)(2,1)S(1)}, u32[]{:S(2)}, u32[]{:S(2)}) collective-permute-start(bf16[1600,128]{1,0:T(8,128)(2,1)S(1)} %collective-permute-done.1.part), channel_id=1, source_target_pairs={{0,1},{1,2},{2,3},{3,4},{4,5},{5,6},{6,7},{7,8},{8,9},{9,10},{10,1... | collective-permute-start | bytes 1228808 | tf_op jit(solution)/shard_map/ppermute | solution.py:227
  143.3 13.4 %collective-permute-start.6 = (bf16[1600,128]{1,0:T(8,128)(2,1)S(1)}, bf16[1600,128]{1,0:T(8,128)(2,1)S(1)}, u32[]{:S(2)}, u32[]{:S(2)}) collective-permute-start(bf16[1600,128]{1,0:T(8,128)(2,1)S(1)} %collective-permute-done.4.part), channel_id=1, source_target_pairs={{0,15},{1,0},{2,1},{3,2},{4,3},{5,4},{6,5},{7,6},{8,7},{9,8},{10,9... | collective-permute-start | bytes 1228808 | tf_op jit(solution)/shard_map/ppermute | solution.py:232
  152.8 12.6 %collective-permute-start.5 = (bf16[1600,128]{1,0:T(8,128)(2,1)S(1)}, bf16[1600,128]{1,0:T(8,128)(2,1)S(1)}, u32[]{:S(2)}, u32[]{:S(2)}) collective-permute-start(bf16[1600,128]{1,0:T(8,128)(2,1)S(1)} %collective-permute-done.3.part), channel_id=1, source_target_pairs={{0,1},{1,2},{2,3},{3,4},{4,5},{5,6},{6,7},{7,8},{8,9},{9,10},{10,1... | collective-permute-start | bytes 1228808 | tf_op jit(solution)/shard_map/ppermute | solution.py:227
Sparse Core Ops, SparseCore 0:
  10.2 82.0 all-gather.2

commit v2 on v1

--- a/solution.py
+++ b/solution.py
@@ -6,6 +6,7 @@
 from jax.experimental import pallas as pl
 from jax.experimental.pallas import tpu as pltpu
 from jax.sharding import PartitionSpec as P
+
 
 EPS = 1e-05
 LANES = 128
@@ -65,15 +66,16 @@
     rows = n * sub
     last = padded - LANES
     gap = frames - last
-    for b in range(last // LANES):
-        block = got_ref[:, :, b * LANES : (b + 1) * LANES]
-        packed_ref[b * rows : (b + 1) * rows, :] = block.reshape(rows, LANES)
+    blocks = [
+        got_ref[:, :, b : b + LANES].reshape(rows, LANES) for b in range(0, last, LANES)
+    ]
     tail = got_ref[:, :, last:].reshape(rows, LANES)
     per = LANES // gap
     depth = rows // per
-    packed_ref[last // LANES * rows :, :] = jnp.concatenate(
-        [tail[q * depth : (q + 1) * depth, :gap] for q in range(per)], axis=1
-    )
+    tail = jnp.concatenate([tail[q * depth : (q + 1) * depth, :gap] for q in range(per)], axis=1)
+    for b, block in enumerate(blocks):
+        packed_ref[b * rows : (b + 1) * rows, :] = block
+    packed_ref[len(blocks) * rows :, :] = tail
     me = where_ref[0]
     block = where_ref[1]
     flags = got_ref[:, 0, last:].astype(jnp.float32)[:, gap : gap + n]
@@ -106,8 +108,11 @@
     ids_ref[0] = ids[:, : ids_ref.shape[2]]
 
 
-def strip_kernel(scale, frames, offset, where_ref, code_ref, part, cols_ref, _, out_ref, prod_ref):
-    n = cols_ref.shape[0]
+def strip_kernel(
+    scale, frames, offset, where_ref, code_ref, part, mine_ref, other_ref, _, out_ref, prod_ref
+):
+    chips = mine_ref.shape[0]
+    n = 2 * chips
     slots = out_ref.shape[0]
     rows = prod_ref.shape[0] // (n + 1)
     sub = rows // n
@@ -119,12 +124,14 @@
     pieces.append(jnp.concatenate([tail[:, q : q + gap] for q in range(0, LANES, gap)], axis=0))
     left = jnp.concatenate(pieces, axis=1)
     prod_ref[n * rows : n * rows + sub, :] = jnp.zeros((sub, LANES), jnp.float32)
-    for g in range(n // 2):
-        pair = jnp.concatenate([cols_ref[2 * g], cols_ref[2 * g + 1]], axis=1)
+    chip, core = where_ref[0] // 2, where_ref[0] % 2
+    for m, away in enumerate(aways(chips)):
+        pair = jnp.concatenate([mine_ref[m], other_ref[m]], axis=1)
         prod = jnp.dot(left, pair, preferred_element_type=jnp.float32)
-        for h in range(2):
-            at = (2 * g + h) * rows
-            prod_ref[at : at + rows, :] = prod[:, h * LANES : (h + 1) * LANES]
+        first = lax.rem(chip + (away + chips), chips) * 2
+        for h, j in enumerate((first + core, first + 1 - core)):
+            at = pl.multiple_of(j * rows, rows)
+            prod_ref[pl.ds(at, rows), :] = prod[:, h * LANES : (h + 1) * LANES]
     group = lax.rem(where_ref[1] + (offset + groups), groups)
     into = pl.ds(pl.multiple_of(group * sub, sub), sub)
     for s in range(slots):
@@ -136,19 +143,33 @@
     return pltpu.with_memory_space_constraint(x, pltpu.VMEM)
 
 
-def strips(part, offset, where, code, cols, out, scale):
-    n, frames, _ = cols.shape
+def in_hbm(x):
+    return pltpu.with_memory_space_constraint(x, pltpu.HBM)
+
+
+def strips(part, offset, where, code, mine, other, out, scale):
+    chips, frames, _ = mine.shape
     rows = part.shape[0] * LANES // frames
     return pl.pallas_call(
         functools.partial(strip_kernel, scale, frames, offset),
         out_shape=pltpu.VMEM(out.shape, out.dtype),
-        in_specs=[SMEM, SMEM, VMEM, VMEM, VMEM],
-        out_specs=VMEM,
-        input_output_aliases={4: 0},
-        scratch_shapes=[pltpu.VMEM(((n + 1) * rows, LANES), jnp.float32)],
+        in_specs=[SMEM, SMEM] + [VMEM] * 4,
+        out_specs=VMEM,
+        input_output_aliases={5: 0},
+        scratch_shapes=[pltpu.VMEM(((2 * chips + 1) * rows, LANES), jnp.float32)],
         compiler_params=pltpu.CompilerParams(vmem_limit_bytes=VMEM_LIMIT),
         name="strips",
-    )(where, code, in_vmem(part), in_vmem(cols), in_vmem(out))
+    )(where, code, in_vmem(part), in_vmem(mine), in_vmem(other), in_vmem(out))
+
+
+def aways(chips):
+    return [-m for m in range(chips // 2 + 1)] + list(range(1, (chips + 1) // 2))
+
+
+def stack_kernel(*refs):
+    *parts, out_ref = refs
+    for m, part in enumerate(parts):
+        out_ref[m] = part[...]
 
 
 def alloc(shape, dtype):
@@ -164,7 +185,7 @@
     )()
 
 
-def shards(series, keep_mask, row_owner):
+def gathered(series, keep_mask, row_owner):
     frames = series.shape[0]
     n_row = lax.axis_size("row")
     n_col = lax.axis_size("col")
@@ -180,61 +201,99 @@
     bf16 = jnp.bfloat16
     sds = jax.ShapeDtypeStruct
 
+    small = pltpu.CompilerParams(vmem_limit_bytes=VMEM_LIMIT)
     scored, chunks = pl.pallas_call(
         score_kernel,
-        out_shape=(sds((frames, LANES), bf16), sds((n_col, sub, padded), bf16)),
+        out_shape=(pltpu.VMEM((frames, LANES), bf16), pltpu.VMEM((n_col, sub, padded), bf16)),
         in_specs=[VMEM],
         out_specs=(VMEM, VMEM),
+        compiler_params=small,
         name="score",
     )(series)
 
+    right = [(i, (i + 2) % n_row) for i in range(n_row)]
+    left = [(i, (i - 2) % n_row) for i in range(n_row)]
+    swap = [(i, i ^ 1) for i in range(n_row)]
+    chips = n_row // 2
     mixed = lax.all_to_all(chunks, "col", 0, 0, tiled=True)
+    hops = {"right": [scored], "left": [scored]}
+
+    def hop(way, perm):
+        hops[way].append(lax.ppermute(hops[way][-1], "row", perm))
+
+    for step in range(1, chips // 2):
+        hop("right", right)
+        if step < chips // 2 - 1:
+            hop("left", left)
     routed = pl.pallas_call(
         functools.partial(route_kernel, frames),
-        out_shape=sds((n_row, sub, padded), bf16),
+        out_shape=pltpu.VMEM((n_row, sub, padded), bf16),
         in_specs=[SMEM, SMEM, VMEM, VMEM],
         out_specs=VMEM,
+        compiler_params=small,
         name="route",
-    )(where, row_owner, mixed, keep_mask)
+    )(where, in_hbm(row_owner), in_vmem(mixed), in_hbm(keep_mask))
     got = lax.all_to_all(routed, "row", 0, 0, tiled=True)
+    long = frames * n_row * sub // LANES
     packed, code, ids = pl.pallas_call(
         functools.partial(pack_kernel, frames),
         out_shape=(
-            sds((frames * n_row * sub // LANES, LANES), bf16),
+            pltpu.VMEM((long, LANES), bf16),
             sds((ALIGN, LANES), jnp.int32),
             sds((1, 1, capacity), jnp.int32),
         ),
         in_specs=[SMEM, VMEM, VMEM],
-        out_specs=(VMEM, VMEM, VMEM),
+        out_specs=(VMEM,) * 3,
+        compiler_params=small,
         name="pack",
-    )(where, got, row_owner.reshape(n_row, row_count))
-
-    cols = lax.all_gather(scored, "row", axis=0, tiled=False)
+    )(where, in_vmem(got), row_owner.reshape(n_row, row_count))
+
+    ring_right = [(i, (i + 1) % n_col) for i in range(n_col)]
+    ring_left = [(i, (i - 1) % n_col) for i in range(n_col)]
+    a = lax.ppermute(packed, "col", ring_right)
+    b = lax.ppermute(packed, "col", ring_left)
+
+    hops["right"][-1], hops["left"][-1], packed = lax.optimization_barrier(
+        (hops["right"][-1], hops["left"][-1], packed)
+    )
+    hop("right", right)
+    hop("left", left)
+    mine = pl.pallas_call(
+        stack_kernel,
+        out_shape=pltpu.VMEM((chips, frames, LANES), bf16),
+        in_specs=[VMEM] * chips,
+        out_specs=VMEM,
+        compiler_params=small,
+        name="stack",
+    )(*map(in_vmem, hops["right"] + hops["left"][1:]))
+    other = lax.ppermute(mine, "row", swap)
 
     out = alloc((capacity, LANES, LANES), bf16)
-    cols = in_vmem(cols)
-    fill = functools.partial(strips, where=where, code=code, cols=cols, scale=1.0 / frames)
-    right = [(i, (i + 1) % n_col) for i in range(n_col)]
-    left = [(i, (i - 1) % n_col) for i in range(n_col)]
+    fill = functools.partial(
+        strips, where=where, code=code, mine=mine, other=other, scale=1.0 / frames
+    )
     half = groups // 2
-    a = lax.ppermute(packed, "col", right)
-    b = lax.ppermute(packed, "col", left)
-    out = fill(packed, 0, out=out)
-    for step in range(1, half + 1):
-        here, there = a, b
+    waiting = [(packed, 0), (a, -1), (b, 1)]
+    for step in range(2, half + 1):
+        if step > 2:
+            out = fill(*waiting.pop(0), out=out)
+            a, out = lax.optimization_barrier((a, out))
+        a = lax.ppermute(a, "col", ring_right)
+        waiting.append((a, -step))
         if step < half:
-            here, out = lax.optimization_barrier((here, out))
-            a = lax.ppermute(here, "col", right)
-        out = fill(here, -step, out=out)
-        if step < half:
-            if step < half - 1:
-                there, out = lax.optimization_barrier((there, out))
-                b = lax.ppermute(there, "col", left)
-            out = fill(there, step, out=out)
+            if step > 2:
+                out = fill(*waiting.pop(0), out=out)
+                b, out = lax.optimization_barrier((b, out))
+            b = lax.ppermute(b, "col", ring_left)
+            waiting.append((b, step))
+    for part, offset in waiting:
+        out = fill(part, offset, out=out)
     return out.reshape(1, 1, capacity, LANES, LANES), ids
 
 
 def solution(mesh):
     in_specs = (P(None, ("subj", "row", "col")), P(("subj", "row"), "col"), P("subj"))
     out_specs = (P(("subj", "row"), "col", None, None, None), P(("subj", "row"), "col", None))
-    return jax.shard_map(shards, mesh=mesh, in_specs=in_specs, out_specs=out_specs, check_vma=False)
+    return jax.shard_map(
+        gathered, mesh=mesh, in_specs=in_specs, out_specs=out_specs, check_vma=False
+    )

time: 178 us -> 194 us (1.090)
  starting transfers between devices: 81.1 us -> 109 us
  between operations: 14.3 us -> 0.9 us
  waiting for transfers between devices: 50.1 us -> 57.5 us
  local copies, waits for them, and re-layouts: 7.06 us -> 2.74 us
  Pallas kernels: 22.8 us -> 20.4 us
    ppermute x7 -> x15, starting transfers between devices: 22.4 us -> 50.1 us  [the longest x7 21.6 us: hop(): hops[way].append(lax.ppermute(hops[way][-1], 'row', perm))]
    ppermute x7 -> x15, waiting for transfers between devices: 14.8 us -> 37 us  [the longest x7 20.2 us: hop(): hops[way].append(lax.ppermute(hops[way][-1], 'row', perm))]
    all_to_all x2, waiting for transfers between devices: 35.2 us -> 20.6 us  [the longest x1 20.6 us: gathered(): mixed = lax.all_to_all(chunks, 'col', 0, 0, tiled=True)]
    unnamed x17 -> x5, local copies, waits for them, and re-layouts: 6.39 us -> 2.67 us
    pallas_call x3 -> x4, Pallas kernels: 6.24 us -> 4.29 us  [the longest x1 1.58 us: gathered(): pl.pallas_call(functools.partial(route_kernel, frames), out_shape=pltpu.V...]
  transfers between devices with their start and end apart: 10 -> 17, of which waited for: 6 -> 10; matrix products, arithmetic and copies ran while one was open for 1% -> 0% of each run, Pallas kernels for 11% -> 8%
where the time goes in v2:
time: 194 us; the launch traced here: 190 us
  starting transfers between devices  109 us (56%)
  waiting for transfers between devices  57.5 us (30%)
  Pallas kernels  20.4 us (11%)
  local copies, waits for them, and re-layouts  2.74 us (1%)
    all_to_all x1, starting transfers between devices, gathered(): mixed = lax.all_to_all(chunks, 'col', 0, 0, tiled=True)  44.2 us
    ppermute x7, starting transfers between devices, hop(): hops[way].append(lax.ppermute(hops[way][-1], 'row', perm))  21.6 us
    all_to_all x1, waiting for transfers between devices, gathered(): mixed = lax.all_to_all(chunks, 'col', 0, 0, tiled=True)  20.6 us
    ppermute x7, waiting for transfers between devices, hop(): hops[way].append(lax.ppermute(hops[way][-1], 'row', perm))  20.2 us
    pallas_call x8, Pallas kernels, strips(): pl.pallas_call(functools.partial(strip_kernel, scale, frames, offset), ou...  16.1 us
    all_to_all x1, starting transfers between devices, gathered(): got = lax.all_to_all(routed, 'row', 0, 0, tiled=True)  14.4 us
    ppermute x2, starting transfers between devices, gathered(): b = lax.ppermute(b, 'col', ring_left)  9.2 us
    ppermute x3, waiting for transfers between devices, gathered(): a = lax.ppermute(a, 'col', ring_right)  8.87 us
  transfers between devices with their start and end apart: 17, of which 10 were waited for; matrix products, arithmetic and copies ran while one was open for 0% of the time, Pallas kernels for 8%

profile of v2, /device:TPU:65, one launch (start us, length us, event | category | flops | bytes accessed | tf_op | source)
XLA Modules:
  0.0 190.3 jit_solution(17542009635584082354)
XLA Ops:
  2.8 44.2 %all-to-all-start = ((bf16[16,16,896]{2,1,0:T(8,128)(2,1)}), bf16[16,16,896]{2,1,0:T(8,128)(2,1)S(1)}, u32[]{:S(2)}, u32[]{:S(2)}) async-start(bf16[16,16,896]{2,1,0:T(8,128)(2,1)} %get-tuple-element.16), calls=%async_computation | async-start | bytes 917504 | tf_op jit(solution)/shard_map/all_to_all | solution.py:218
  47.1 20.6 %all-to-all-done.chunks_ref = bf16[16,16,896]{2,1,0:T(8,128)(2,1)S(1)} async-done(((bf16[16,16,896]{2,1,0:T(8,128)(2,1)}), bf16[16,16,896]{2,1,0:T(8,128)(2,1)S(1)}, u32[]{:S(2)}, u32[]{:S(2)}) %all-to-all-start) | async-done | bytes 458784 | tf_op jit(solution)/shard_map/all_to_all | solution.py:218
  69.2 14.4 %all-to-all-start.1 = ((bf16[16,16,896]{2,1,0:T(8,128)(2,1)}), bf16[16,16,896]{2,1,0:T(8,128)(2,1)S(1)}, u32[]{:S(2)}, u32[]{:S(2)}) async-start(bf16[16,16,896]{2,1,0:T(8,128)(2,1)} %route.1), calls=%async_computation.1 | async-start | bytes 917504 | tf_op jit(solution)/shard_map/all_to_all | solution.py:236
  83.6 3.3 %collective-permute-start.2 = (bf16[800,128]{1,0:T(8,128)(2,1)S(1)}, bf16[800,128]{1,0:T(8,128)(2,1)S(1)}, u32[]{:S(2)}, u32[]{:S(2)}) collective-permute-start(bf16[800,128]{1,0:T(8,128)(2,1)S(1)} %get-tuple-element.19.refs_0_), channel_id=1, source_target_pairs={{0,32},{16,48},{32,64},{48,80},{64,96},{80,112},{96,128},{112,144}... | collective-permute-start | bytes 614408 | tf_op jit(solution)/shard_map/ppermute | solution.py:222
  86.9 3.3 %collective-permute-start.5 = (bf16[800,128]{1,0:T(8,128)(2,1)S(1)}, bf16[800,128]{1,0:T(8,128)(2,1)S(1)}, u32[]{:S(2)}, u32[]{:S(2)}) collective-permute-start(bf16[800,128]{1,0:T(8,128)(2,1)S(1)} %get-tuple-element.19.refs_0_), channel_id=1, source_target_pairs={{0,224},{16,240},{32,0},{48,16},{64,32},{80,48},{96,64},{112,80},{... | collective-permute-start | bytes 614408 | tf_op jit(solution)/shard_map/ppermute | solution.py:222
  90.2 11.1 %collective-permute-done.2.refs_1_ = bf16[800,128]{1,0:T(8,128)(2,1)S(1)} collective-permute-done((bf16[800,128]{1,0:T(8,128)(2,1)S(1)}, bf16[800,128]{1,0:T(8,128)(2,1)S(1)}, u32[]{:S(2)}, u32[]{:S(2)}) %collective-permute-start.2) | collective-permute-done | bytes 204832 | tf_op jit(solution)/shard_map/ppermute | solution.py:222
  103.2 4.6 %collective-permute-start.6 = (bf16[800,128]{1,0:T(8,128)(2,1)S(1)}, bf16[800,128]{1,0:T(8,128)(2,1)S(1)}, u32[]{:S(2)}, u32[]{:S(2)}) collective-permute-start(bf16[800,128]{1,0:T(8,128)(2,1)S(1)} %collective-permute-done.5.refs_5_), channel_id=1, source_target_pairs={{0,224},{16,240},{32,0},{48,16},{64,32},{80,48},{96,64},{112,80},{... | collective-permute-start | bytes 614408 | tf_op jit(solution)/shard_map/ppermute | solution.py:222
  107.9 2.2 %collective-permute-done.3.refs_2_ = bf16[800,128]{1,0:T(8,128)(2,1)S(1)} collective-permute-done((bf16[800,128]{1,0:T(8,128)(2,1)S(1)}, bf16[800,128]{1,0:T(8,128)(2,1)S(1)}, u32[]{:S(2)}, u32[]{:S(2)}) %collective-permute-start.3) | collective-permute-done | bytes 204832 | tf_op jit(solution)/shard_map/ppermute | solution.py:222
  113.6 4.2 %collective-permute-done.4.refs_3_ = bf16[800,128]{1,0:T(8,128)(2,1)S(1)} collective-permute-done((bf16[800,128]{1,0:T(8,128)(2,1)S(1)}, bf16[800,128]{1,0:T(8,128)(2,1)S(1)}, u32[]{:S(2)}, u32[]{:S(2)}) %collective-permute-start.4) | collective-permute-done | bytes 204832 | tf_op jit(solution)/shard_map/ppermute | solution.py:222
  119.8 4.6 %collective-permute-start.8 = (bf16[800,128]{1,0:T(8,128)(2,1)S(1)}, bf16[800,128]{1,0:T(8,128)(2,1)S(1)}, u32[]{:S(2)}, u32[]{:S(2)}) collective-permute-start(bf16[800,128]{1,0:T(8,128)(2,1)S(1)} %collective-permute-done.6.refs_6_), channel_id=1, source_target_pairs={{0,224},{16,240},{32,0},{48,16},{64,32},{80,48},{96,64},{112,80},{... | collective-permute-start | bytes 614408 | tf_op jit(solution)/shard_map/ppermute | solution.py:222
  127.2 6.0 %collective-permute-start.9 = (bf16[8,800,128]{2,1,0:T(8,128)(2,1)S(1)}, bf16[8,800,128]{2,1,0:T(8,128)(2,1)S(1)}, u32[]{:S(2)}, u32[]{:S(2)}) collective-permute-start(bf16[8,800,128]{2,1,0:T(8,128)(2,1)S(1)} %stack.13.mine_ref), channel_id=1, source_target_pairs={{0,16},{16,0},{32,48},{48,32},{64,80},{80,64},{96,112},{112,96},{1... | collective-permute-start | bytes 4915208 | tf_op jit(solution)/shard_map/ppermute | solution.py:269
  135.2 5.5 %collective-permute-start.11 = (bf16[1600,128]{1,0:T(8,128)(2,1)S(1)}, bf16[1600,128]{1,0:T(8,128)(2,1)S(1)}, u32[]{:S(2)}, u32[]{:S(2)}) collective-permute-start(bf16[1600,128]{1,0:T(8,128)(2,1)S(1)} %get-tuple-element.20.part), channel_id=1, source_target_pairs={{0,15},{1,0},{2,1},{3,2},{4,3},{5,4},{6,5},{7,6},{8,7},{9,8},{10,9... | collective-permute-start | bytes 1228808 | tf_op jit(solution)/shard_map/ppermute | solution.py:254
  140.7 7.9 %collective-permute-done.part = bf16[1600,128]{1,0:T(8,128)(2,1)S(1)} collective-permute-done((bf16[1600,128]{1,0:T(8,128)(2,1)S(1)}, bf16[1600,128]{1,0:T(8,128)(2,1)S(1)}, u32[]{:S(2)}, u32[]{:S(2)}) %collective-permute-start) | collective-permute-done | bytes 409632 | tf_op jit(solution)/shard_map/ppermute | solution.py:253
  150.5 4.6 %collective-permute-start.12 = (bf16[1600,128]{1,0:T(8,128)(2,1)S(1)}, bf16[1600,128]{1,0:T(8,128)(2,1)S(1)}, u32[]{:S(2)}, u32[]{:S(2)}) collective-permute-start(bf16[1600,128]{1,0:T(8,128)(2,1)S(1)} %collective-permute-done.11.part), channel_id=1, source_target_pairs={{0,15},{1,0},{2,1},{3,2},{4,3},{5,4},{6,5},{7,6},{8,7},{9,8},{10,9... | collective-permute-start | bytes 1228808 | tf_op jit(solution)/shard_map/ppermute | solution.py:287
  155.1 2.0 %strips.8._ = bf16[96,128,128]{2,1,0:T(8,128)(2,1)S(1)} custom-call(s32[2]{0:T(128)S(1)} %pad_add_fusion.where_ref, s32[8,128]{1,0:T(8,128)S(1)} %get-tuple-element.17.code_ref, bf16[1600,128]{1,0:T(8,128)(2,1)S(1)} %get-tuple-element.20.part, bf16[8,800,128]{2,1,0:T(8,128)(2,1)S(1)} %stack.13.mine_ref, ...), custom_call_target="tpu_custom_call", output_to_operand_aliasing={{}: (5, {})} | custom-call | tf_op jit(solution)/shard_map/strips/pallas_call | solution.py:153
  157.1 5.0 %collective-permute-done.1.part = bf16[1600,128]{1,0:T(8,128)(2,1)S(1)} collective-permute-done((bf16[1600,128]{1,0:T(8,128)(2,1)S(1)}, bf16[1600,128]{1,0:T(8,128)(2,1)S(1)}, u32[]{:S(2)}, u32[]{:S(2)}) %collective-permute-start.1) | collective-permute-done | bytes 409632 | tf_op jit(solution)/shard_map/ppermute | solution.py:281
  164.0 2.0 %strips.9._ = bf16[96,128,128]{2,1,0:T(8,128)(2,1)S(1)} custom-call(s32[2]{0:T(128)S(1)} %pad_add_fusion.where_ref, s32[8,128]{1,0:T(8,128)S(1)} %get-tuple-element.17.code_ref, bf16[1600,128]{1,0:T(8,128)(2,1)S(1)} %collective-permute-done.part, bf16[8,800,128]{2,1,0:T(8,128)(2,1)S(1)} %stack.13.mine_ref, ...), custom_call_target="tpu_custom_call", output_to_operand_aliasing={{}: (5, {})} | custom-call | tf_op jit(solution)/shard_map/strips/pallas_call | solution.py:153
  166.0 4.6 %collective-permute-start.14 = (bf16[1600,128]{1,0:T(8,128)(2,1)S(1)}, bf16[1600,128]{1,0:T(8,128)(2,1)S(1)}, u32[]{:S(2)}, u32[]{:S(2)}) collective-permute-start(bf16[1600,128]{1,0:T(8,128)(2,1)S(1)} %collective-permute-done.12.part), channel_id=1, source_target_pairs={{0,15},{1,0},{2,1},{3,2},{4,3},{5,4},{6,5},{7,6},{8,7},{9,8},{10,9... | collective-permute-start | bytes 1228808 | tf_op jit(solution)/shard_map/ppermute | solution.py:287
  170.7 2.0 %strips.10._ = bf16[96,128,128]{2,1,0:T(8,128)(2,1)S(1)} custom-call(s32[2]{0:T(128)S(1)} %pad_add_fusion.where_ref, s32[8,128]{1,0:T(8,128)S(1)} %get-tuple-element.17.code_ref, bf16[1600,128]{1,0:T(8,128)(2,1)S(1)} %collective-permute-done.11.part, bf16[8,800,128]{2,1,0:T(8,128)(2,1)S(1)} %stack.13.mine_ref, ...), custom_call_target="tpu_custom_call", output_to_operand_aliasing={{}: (5, {})} | custom-call | tf_op jit(solution)/shard_map/strips/pallas_call | solution.py:153
  172.7 2.1 %collective-permute-done.10.part = bf16[1600,128]{1,0:T(8,128)(2,1)S(1)} collective-permute-done((bf16[1600,128]{1,0:T(8,128)(2,1)S(1)}, bf16[1600,128]{1,0:T(8,128)(2,1)S(1)}, u32[]{:S(2)}, u32[]{:S(2)}) %collective-permute-start.10) | collective-permute-done | bytes 409632 | tf_op jit(solution)/shard_map/ppermute | solution.py:281
  176.7 2.0 %strips.11._ = bf16[96,128,128]{2,1,0:T(8,128)(2,1)S(1)} custom-call(s32[2]{0:T(128)S(1)} %pad_add_fusion.where_ref, s32[8,128]{1,0:T(8,128)S(1)} %get-tuple-element.17.code_ref, bf16[1600,128]{1,0:T(8,128)(2,1)S(1)} %collective-permute-done.1.part, bf16[8,800,128]{2,1,0:T(8,128)(2,1)S(1)} %stack.13.mine_ref, ...), custom_call_target="tpu_custom_call", output_to_operand_aliasing={{}: (5, {})} | custom-call | tf_op jit(solution)/shard_map/strips/pallas_call | solution.py:153
  178.7 2.0 %strips.12._ = bf16[96,128,128]{2,1,0:T(8,128)(2,1)S(1)} custom-call(s32[2]{0:T(128)S(1)} %pad_add_fusion.where_ref, s32[8,128]{1,0:T(8,128)S(1)} %get-tuple-element.17.code_ref, bf16[1600,128]{1,0:T(8,128)(2,1)S(1)} %collective-permute-done.12.part, bf16[8,800,128]{2,1,0:T(8,128)(2,1)S(1)} %stack.13.mine_ref, ...), custom_call_target="tpu_custom_call", output_to_operand_aliasing={{}: (5, {})} | custom-call | tf_op jit(solution)/shard_map/strips/pallas_call | solution.py:153
  180.7 2.0 %strips.13._ = bf16[96,128,128]{2,1,0:T(8,128)(2,1)S(1)} custom-call(s32[2]{0:T(128)S(1)} %pad_add_fusion.where_ref, s32[8,128]{1,0:T(8,128)S(1)} %get-tuple-element.17.code_ref, bf16[1600,128]{1,0:T(8,128)(2,1)S(1)} %collective-permute-done.10.part, bf16[8,800,128]{2,1,0:T(8,128)(2,1)S(1)} %stack.13.mine_ref, ...), custom_call_target="tpu_custom_call", output_to_operand_aliasing={{}: (5, {})} | custom-call | tf_op jit(solution)/shard_map/strips/pallas_call | solution.py:153
  182.8 2.0 %strips.14._ = bf16[96,128,128]{2,1,0:T(8,128)(2,1)S(1)} custom-call(s32[2]{0:T(128)S(1)} %pad_add_fusion.where_ref, s32[8,128]{1,0:T(8,128)S(1)} %get-tuple-element.17.code_ref, bf16[1600,128]{1,0:T(8,128)(2,1)S(1)} %collective-permute-done.14.part, bf16[8,800,128]{2,1,0:T(8,128)(2,1)S(1)} %stack.13.mine_ref, ...), custom_call_target="tpu_custom_call", output_to_operand_aliasing={{}: (5, {})} | custom-call | tf_op jit(solution)/shard_map/strips/pallas_call | solution.py:153
  (30 shorter events, 27.2 us)
Async XLA Ops:
  0.6 1.0 copy-start
  1.6 110.4 %copy-start.1 = (s32[256]{0:T(256)S(1)}, s32[256]{0:T(256)}, u32[]{:S(2)}) copy-start(s32[256]{0:T(256)} %owner_ref.1) | copy-start | bytes 3076
  2.8 64.9 %all-to-all-start = ((bf16[16,16,896]{2,1,0:T(8,128)(2,1)}), bf16[16,16,896]{2,1,0:T(8,128)(2,1)S(1)}, u32[]{:S(2)}, u32[]{:S(2)}) async-start(bf16[16,16,896]{2,1,0:T(8,128)(2,1)} %get-tuple-element.16), calls=%async_computation | async-start | bytes 917504 | tf_op jit(solution)/shard_map/all_to_all | solution.py:218
  69.2 42.9 %all-to-all-start.1 = ((bf16[16,16,896]{2,1,0:T(8,128)(2,1)}), bf16[16,16,896]{2,1,0:T(8,128)(2,1)S(1)}, u32[]{:S(2)}, u32[]{:S(2)}) async-start(bf16[16,16,896]{2,1,0:T(8,128)(2,1)} %route.1), calls=%async_computation.1 | async-start | bytes 917504 | tf_op jit(solution)/shard_map/all_to_all | solution.py:236
  83.6 17.7 %collective-permute-start.2 = (bf16[800,128]{1,0:T(8,128)(2,1)S(1)}, bf16[800,128]{1,0:T(8,128)(2,1)S(1)}, u32[]{:S(2)}, u32[]{:S(2)}) collective-permute-start(bf16[800,128]{1,0:T(8,128)(2,1)S(1)} %get-tuple-element.19.refs_0_), channel_id=1, source_target_pairs={{0,32},{16,48},{32,64},{48,80},{64,96},{80,112},{96,128},{112,144}... | collective-permute-start | bytes 614408 | tf_op jit(solution)/shard_map/ppermute | solution.py:222
  86.9 16.3 %collective-permute-start.5 = (bf16[800,128]{1,0:T(8,128)(2,1)S(1)}, bf16[800,128]{1,0:T(8,128)(2,1)S(1)}, u32[]{:S(2)}, u32[]{:S(2)}) collective-permute-start(bf16[800,128]{1,0:T(8,128)(2,1)S(1)} %get-tuple-element.19.refs_0_), channel_id=1, source_target_pairs={{0,224},{16,240},{32,0},{48,16},{64,32},{80,48},{96,64},{112,80},{... | collective-permute-start | bytes 614408 | tf_op jit(solution)/shard_map/ppermute | solution.py:222
  101.3 8.8 %collective-permute-start.3 = (bf16[800,128]{1,0:T(8,128)(2,1)S(1)}, bf16[800,128]{1,0:T(8,128)(2,1)S(1)}, u32[]{:S(2)}, u32[]{:S(2)}) collective-permute-start(bf16[800,128]{1,0:T(8,128)(2,1)S(1)} %collective-permute-done.2.refs_1_), channel_id=1, source_target_pairs={{0,32},{16,48},{32,64},{48,80},{64,96},{80,112},{96,128},{112,144}... | collective-permute-start | bytes 614408 | tf_op jit(solution)/shard_map/ppermute | solution.py:222
  103.2 10.3 %collective-permute-start.6 = (bf16[800,128]{1,0:T(8,128)(2,1)S(1)}, bf16[800,128]{1,0:T(8,128)(2,1)S(1)}, u32[]{:S(2)}, u32[]{:S(2)}) collective-permute-start(bf16[800,128]{1,0:T(8,128)(2,1)S(1)} %collective-permute-done.5.refs_5_), channel_id=1, source_target_pairs={{0,224},{16,240},{32,0},{48,16},{64,32},{80,48},{96,64},{112,80},{... | collective-permute-start | bytes 614408 | tf_op jit(solution)/shard_map/ppermute | solution.py:222
  110.1 7.7 %collective-permute-start.4 = (bf16[800,128]{1,0:T(8,128)(2,1)S(1)}, bf16[800,128]{1,0:T(8,128)(2,1)S(1)}, u32[]{:S(2)}, u32[]{:S(2)}) collective-permute-start(bf16[800,128]{1,0:T(8,128)(2,1)S(1)} %collective-permute-done.3.refs_2_), channel_id=1, source_target_pairs={{0,32},{16,48},{32,64},{48,80},{64,96},{80,112},{96,128},{112,144}... | collective-permute-start | bytes 614408 | tf_op jit(solution)/shard_map/ppermute | solution.py:222
  117.8 7.7 %collective-permute-start.7 = (bf16[800,128]{1,0:T(8,128)(2,1)S(1)}, bf16[800,128]{1,0:T(8,128)(2,1)S(1)}, u32[]{:S(2)}, u32[]{:S(2)}) collective-permute-start(bf16[800,128]{1,0:T(8,128)(2,1)S(1)} %collective-permute-done.4.refs_3_), channel_id=1, source_target_pairs={{0,32},{16,48},{32,64},{48,80},{64,96},{80,112},{96,128},{112,144}... | collective-permute-start | bytes 614408 | tf_op jit(solution)/shard_map/ppermute | solution.py:222
  119.8 7.3 %collective-permute-start.8 = (bf16[800,128]{1,0:T(8,128)(2,1)S(1)}, bf16[800,128]{1,0:T(8,128)(2,1)S(1)}, u32[]{:S(2)}, u32[]{:S(2)}) collective-permute-start(bf16[800,128]{1,0:T(8,128)(2,1)S(1)} %collective-permute-done.6.refs_6_), channel_id=1, source_target_pairs={{0,224},{16,240},{32,0},{48,16},{64,32},{80,48},{96,64},{112,80},{... | collective-permute-start | bytes 614408 | tf_op jit(solution)/shard_map/ppermute | solution.py:222
  127.2 27.9 %collective-permute-start.9 = (bf16[8,800,128]{2,1,0:T(8,128)(2,1)S(1)}, bf16[8,800,128]{2,1,0:T(8,128)(2,1)S(1)}, u32[]{:S(2)}, u32[]{:S(2)}) collective-permute-start(bf16[8,800,128]{2,1,0:T(8,128)(2,1)S(1)} %stack.13.mine_ref), channel_id=1, source_target_pairs={{0,16},{16,0},{32,48},{48,32},{64,80},{80,64},{96,112},{112,96},{1... | collective-permute-start | bytes 4915208 | tf_op jit(solution)/shard_map/ppermute | solution.py:269
  133.2 15.3 %collective-permute-start = (bf16[1600,128]{1,0:T(8,128)(2,1)S(1)}, bf16[1600,128]{1,0:T(8,128)(2,1)S(1)}, u32[]{:S(2)}, u32[]{:S(2)}) collective-permute-start(bf16[1600,128]{1,0:T(8,128)(2,1)S(1)} %get-tuple-element.20.part), channel_id=1, source_target_pairs={{0,1},{1,2},{2,3},{3,4},{4,5},{5,6},{6,7},{7,8},{8,9},{9,10},{10,1... | collective-permute-start | bytes 1228808 | tf_op jit(solution)/shard_map/ppermute | solution.py:253
  135.2 15.3 %collective-permute-start.11 = (bf16[1600,128]{1,0:T(8,128)(2,1)S(1)}, bf16[1600,128]{1,0:T(8,128)(2,1)S(1)}, u32[]{:S(2)}, u32[]{:S(2)}) collective-permute-start(bf16[1600,128]{1,0:T(8,128)(2,1)S(1)} %get-tuple-element.20.part), channel_id=1, source_target_pairs={{0,15},{1,0},{2,1},{3,2},{4,3},{5,4},{6,5},{7,6},{8,7},{9,8},{10,9... | collective-permute-start | bytes 1228808 | tf_op jit(solution)/shard_map/ppermute | solution.py:254
  148.5 13.6 %collective-permute-start.1 = (bf16[1600,128]{1,0:T(8,128)(2,1)S(1)}, bf16[1600,128]{1,0:T(8,128)(2,1)S(1)}, u32[]{:S(2)}, u32[]{:S(2)}) collective-permute-start(bf16[1600,128]{1,0:T(8,128)(2,1)S(1)} %collective-permute-done.part), channel_id=1, source_target_pairs={{0,1},{1,2},{2,3},{3,4},{4,5},{5,6},{6,7},{7,8},{8,9},{9,10},{10,1... | collective-permute-start | bytes 1228808 | tf_op jit(solution)/shard_map/ppermute | solution.py:281
  150.5 15.6 %collective-permute-start.12 = (bf16[1600,128]{1,0:T(8,128)(2,1)S(1)}, bf16[1600,128]{1,0:T(8,128)(2,1)S(1)}, u32[]{:S(2)}, u32[]{:S(2)}) collective-permute-start(bf16[1600,128]{1,0:T(8,128)(2,1)S(1)} %collective-permute-done.11.part), channel_id=1, source_target_pairs={{0,15},{1,0},{2,1},{3,2},{4,3},{5,4},{6,5},{7,6},{8,7},{9,8},{10,9... | collective-permute-start | bytes 1228808 | tf_op jit(solution)/shard_map/ppermute | solution.py:287
  162.1 12.7 %collective-permute-start.10 = (bf16[1600,128]{1,0:T(8,128)(2,1)S(1)}, bf16[1600,128]{1,0:T(8,128)(2,1)S(1)}, u32[]{:S(2)}, u32[]{:S(2)}) collective-permute-start(bf16[1600,128]{1,0:T(8,128)(2,1)S(1)} %collective-permute-done.1.part), channel_id=1, source_target_pairs={{0,1},{1,2},{2,3},{3,4},{4,5},{5,6},{6,7},{7,8},{8,9},{9,10},{10,1... | collective-permute-start | bytes 1228808 | tf_op jit(solution)/shard_map/ppermute | solution.py:281
  166.0 16.7 %collective-permute-start.14 = (bf16[1600,128]{1,0:T(8,128)(2,1)S(1)}, bf16[1600,128]{1,0:T(8,128)(2,1)S(1)}, u32[]{:S(2)}, u32[]{:S(2)}) collective-permute-start(bf16[1600,128]{1,0:T(8,128)(2,1)S(1)} %collective-permute-done.12.part), channel_id=1, source_target_pairs={{0,15},{1,0},{2,1},{3,2},{4,3},{5,4},{6,5},{7,6},{8,7},{9,8},{10,9... | collective-permute-start | bytes 1228808 | tf_op jit(solution)/shard_map/ppermute | solution.py:287
  174.8 11.8 %collective-permute-start.13 = (bf16[1600,128]{1,0:T(8,128)(2,1)S(1)}, bf16[1600,128]{1,0:T(8,128)(2,1)S(1)}, u32[]{:S(2)}, u32[]{:S(2)}) collective-permute-start(bf16[1600,128]{1,0:T(8,128)(2,1)S(1)} %collective-permute-done.10.part), channel_id=1, source_target_pairs={{0,1},{1,2},{2,3},{3,4},{4,5},{5,6},{6,7},{7,8},{8,9},{9,10},{10,1... | collective-permute-start | bytes 1228808 | tf_op jit(solution)/shard_map/ppermute | solution.py:281

commit v3 on v2

--- a/solution.py
+++ b/solution.py
@@ -39,7 +39,7 @@
             chunks_ref[at : at + groups, :, b * LANES : (b + 1) * LANES] = flipped
 
 
-def route_kernel(frames, where_ref, owner_ref, chunks_ref, keep_ref, out_ref):
+def route_kernel(frames, owner_ref, chunks_ref, keep_ref, out_ref):
     n = chunks_ref.shape[0]
     padded = chunks_ref.shape[2]
     last = padded - LANES
@@ -53,7 +53,7 @@
         ],
         axis=1,
     )
-    base = where_ref[0] * n
+    base = lax.axis_index("row") * n
     for k in range(n):
         owner = owner_ref[base + k]
         out_ref[owner, :, :last] = chunks_ref[k, :, :last]
@@ -61,7 +61,7 @@
         out_ref[owner, :, last:] = tail.astype(jnp.bfloat16)
 
 
-def pack_kernel(frames, where_ref, got_ref, owner_ref, packed_ref, code_ref, ids_ref):
+def pack_kernel(frames, got_ref, packed_ref):
     n, sub, padded = got_ref.shape
     rows = n * sub
     last = padded - LANES
@@ -76,8 +76,15 @@
     for b, block in enumerate(blocks):
         packed_ref[b * rows : (b + 1) * rows, :] = block
     packed_ref[len(blocks) * rows :, :] = tail
-    me = where_ref[0]
-    block = where_ref[1]
+
+
+def list_kernel(frames, got_ref, owner_ref, code_ref, ids_ref):
+    n, sub, padded = got_ref.shape
+    rows = n * sub
+    last = padded - LANES
+    gap = frames - last
+    me = lax.axis_index("row")
+    block = lax.axis_index("col")
     flags = got_ref[:, 0, last:].astype(jnp.float32)[:, gap : gap + n]
     r_of = lax.broadcasted_iota(jnp.int32, (n, n), 0)
     k_of = lax.broadcasted_iota(jnp.int32, (n, n), 1)
@@ -109,7 +116,7 @@
 
 
 def strip_kernel(
-    scale, frames, offset, where_ref, code_ref, part, mine_ref, other_ref, _, out_ref, prod_ref
+    scale, frames, offset, code_ref, part, mine_ref, other_ref, _, out_ref, prod_ref, *last_refs
 ):
     chips = mine_ref.shape[0]
     n = 2 * chips
@@ -124,7 +131,8 @@
     pieces.append(jnp.concatenate([tail[:, q : q + gap] for q in range(0, LANES, gap)], axis=0))
     left = jnp.concatenate(pieces, axis=1)
     prod_ref[n * rows : n * rows + sub, :] = jnp.zeros((sub, LANES), jnp.float32)
-    chip, core = where_ref[0] // 2, where_ref[0] % 2
+    me = lax.axis_index("row")
+    chip, core = me // 2, me % 2
     for m, away in enumerate(aways(chips)):
         pair = jnp.concatenate([mine_ref[m], other_ref[m]], axis=1)
         prod = jnp.dot(left, pair, preferred_element_type=jnp.float32)
@@ -132,11 +140,25 @@
         for h, j in enumerate((first + core, first + 1 - core)):
             at = pl.multiple_of(j * rows, rows)
             prod_ref[pl.ds(at, rows), :] = prod[:, h * LANES : (h + 1) * LANES]
-    group = lax.rem(where_ref[1] + (offset + groups), groups)
+    group = lax.rem(lax.axis_index("col") + (offset + groups), groups)
     into = pl.ds(pl.multiple_of(group * sub, sub), sub)
     for s in range(slots):
         strip = prod_ref[pl.ds(pl.multiple_of(code_ref[0, s], sub), sub), :]
-        out_ref[s, into, :] = (strip * scale).astype(jnp.bfloat16)
+        strip = (strip * scale).astype(jnp.bfloat16)
+        if last_refs:
+            last_refs[0][s] = strip
+        else:
+            out_ref[s, into, :] = strip
+    if last_refs:
+        store = pltpu.make_async_copy(last_refs[0], out_ref.at[:, into, :], last_refs[1])
+        store.start()
+        store.wait()
+
+
+def flush_kernel(filled_ref, out_ref, sem):
+    store = pltpu.make_async_copy(filled_ref, out_ref, sem)
+    store.start()
+    store.wait()
 
 
 def in_vmem(x):
@@ -147,19 +169,33 @@
     return pltpu.with_memory_space_constraint(x, pltpu.HBM)
 
 
-def strips(part, offset, where, code, mine, other, out, scale):
+def strips(part, offset, code, mine, other, out, scale, final=False):
     chips, frames, _ = mine.shape
     rows = part.shape[0] * LANES // frames
+    sub = rows // (2 * chips)
+    scratch = [pltpu.VMEM(((2 * chips + 1) * rows, LANES), jnp.float32)]
+    if final:
+        scratch += [
+            pltpu.VMEM((out.shape[0], sub, LANES), out.dtype),
+            pltpu.SemaphoreType.DMA,
+        ]
+    shape, space = (pltpu.HBM, pl.ANY) if final else (pltpu.VMEM, pltpu.VMEM)
     return pl.pallas_call(
         functools.partial(strip_kernel, scale, frames, offset),
-        out_shape=pltpu.VMEM(out.shape, out.dtype),
-        in_specs=[SMEM, SMEM] + [VMEM] * 4,
-        out_specs=VMEM,
-        input_output_aliases={5: 0},
-        scratch_shapes=[pltpu.VMEM(((2 * chips + 1) * rows, LANES), jnp.float32)],
+        out_shape=shape(out.shape, out.dtype),
+        in_specs=[SMEM] + [VMEM] * 3 + [pl.BlockSpec(memory_space=space)],
+        out_specs=pl.BlockSpec(memory_space=space),
+        input_output_aliases={4: 0},
+        scratch_shapes=scratch,
         compiler_params=pltpu.CompilerParams(vmem_limit_bytes=VMEM_LIMIT),
         name="strips",
-    )(where, code, in_vmem(part), in_vmem(mine), in_vmem(other), in_vmem(out))
+    )(
+        code,
+        in_vmem(part),
+        in_vmem(mine),
+        in_vmem(other),
+        in_hbm(out) if final else in_vmem(out),
+    )
 
 
 def aways(chips):
@@ -195,9 +231,6 @@
     padded = -(-frames // LANES) * LANES
     groups = n_col // COPIES
     sub = LANES // groups
-    my_row = lax.axis_index("row")
-    my_col = lax.axis_index("col")
-    where = jnp.stack([my_row, my_col]).astype(jnp.int32)
     bf16 = jnp.bfloat16
     sds = jax.ShapeDtypeStruct
 
@@ -228,30 +261,38 @@
     routed = pl.pallas_call(
         functools.partial(route_kernel, frames),
         out_shape=pltpu.VMEM((n_row, sub, padded), bf16),
-        in_specs=[SMEM, SMEM, VMEM, VMEM],
+        in_specs=[SMEM, VMEM, VMEM],
         out_specs=VMEM,
         compiler_params=small,
         name="route",
-    )(where, in_hbm(row_owner), in_vmem(mixed), in_hbm(keep_mask))
+    )(in_hbm(row_owner), in_vmem(mixed), in_hbm(keep_mask))
     got = lax.all_to_all(routed, "row", 0, 0, tiled=True)
     long = frames * n_row * sub // LANES
-    packed, code, ids = pl.pallas_call(
+    packed = pl.pallas_call(
         functools.partial(pack_kernel, frames),
-        out_shape=(
-            pltpu.VMEM((long, LANES), bf16),
-            sds((ALIGN, LANES), jnp.int32),
-            sds((1, 1, capacity), jnp.int32),
-        ),
-        in_specs=[SMEM, VMEM, VMEM],
-        out_specs=(VMEM,) * 3,
+        out_shape=pltpu.VMEM((long, LANES), bf16),
+        in_specs=[VMEM],
+        out_specs=VMEM,
         compiler_params=small,
         name="pack",
-    )(where, in_vmem(got), row_owner.reshape(n_row, row_count))
+    )(in_vmem(got))
 
     ring_right = [(i, (i + 1) % n_col) for i in range(n_col)]
     ring_left = [(i, (i - 1) % n_col) for i in range(n_col)]
     a = lax.ppermute(packed, "col", ring_right)
     b = lax.ppermute(packed, "col", ring_left)
+
+    code, ids = pl.pallas_call(
+        functools.partial(list_kernel, frames),
+        out_shape=(
+            sds((ALIGN, LANES), jnp.int32),
+            sds((1, 1, capacity), jnp.int32),
+        ),
+        in_specs=[VMEM, VMEM],
+        out_specs=(VMEM, VMEM),
+        compiler_params=small,
+        name="lists",
+    )(in_vmem(got), row_owner.reshape(n_row, row_count))
 
     hops["right"][-1], hops["left"][-1], packed = lax.optimization_barrier(
         (hops["right"][-1], hops["left"][-1], packed)
@@ -270,7 +311,7 @@
 
     out = alloc((capacity, LANES, LANES), bf16)
     fill = functools.partial(
-        strips, where=where, code=code, mine=mine, other=other, scale=1.0 / frames
+        strips, code=code, mine=mine, other=other, scale=1.0 / frames
     )
     half = groups // 2
     waiting = [(packed, 0), (a, -1), (b, 1)]
@@ -286,8 +327,18 @@
                 b, out = lax.optimization_barrier((b, out))
             b = lax.ppermute(b, "col", ring_left)
             waiting.append((b, step))
-    for part, offset in waiting:
-        out = fill(part, offset, out=out)
+    for part, offset in sorted(waiting, key=lambda item: item[1] == -half):
+        if offset == -half:
+            out = pl.pallas_call(
+                flush_kernel,
+                out_shape=pltpu.HBM(out.shape, out.dtype),
+                in_specs=[VMEM],
+                out_specs=pl.BlockSpec(memory_space=pl.ANY),
+                scratch_shapes=[pltpu.SemaphoreType.DMA],
+                compiler_params=small,
+                name="flush",
+            )(in_vmem(out))
+        out = fill(part, offset, out=out, final=offset == -half)
     return out.reshape(1, 1, capacity, LANES, LANES), ids
 
 

time: 194 us -> 193 us (level)
  blocking collectives: 0 us -> 64.6 us
  starting transfers between devices: 109 us -> 64.5 us
  waiting for transfers between devices: 57.5 us -> 33.4 us
  Pallas kernels: 20.4 us -> 24.1 us
    all_to_all x0 -> x1, blocking collectives: none -> 64.6 us  [gathered(): mixed = lax.all_to_all(chunks, 'col', 0, 0, tiled=True)]
    all_to_all x1 -> x0, starting transfers between devices: 44.2 us -> none  [gathered(): mixed = lax.all_to_all(chunks, 'col', 0, 0, tiled=True)]
    all_to_all x1 -> x0, waiting for transfers between devices: 20.6 us -> none  [gathered(): mixed = lax.all_to_all(chunks, 'col', 0, 0, tiled=True)]
    ppermute x3, waiting for transfers between devices: 8.87 us -> 4.37 us  [gathered(): a = lax.ppermute(a, 'col', ring_right)]
    pallas_call x8, Pallas kernels: 16.1 us -> 18.4 us  [strips(): pl.pallas_call(functools.partial(strip_kernel, scale, frames, offset), ou...]
    pallas_call x1 -> x3, Pallas kernels: 1.47 us -> 3.49 us  [the longest x1 1.67 us: gathered(): pl.pallas_call(flush_kernel, out_shape=pltpu.HBM(out.shape, out.dtype), i...]
  transfers between devices with their start and end apart: 17 -> 16, of which waited for: 10 -> 8; matrix products, arithmetic and copies ran while one was open for 0% -> 0% of each run, Pallas kernels for 8% -> 10%
where the time goes in v3:
time: 193 us; the launch traced here: 190 us
  blocking collectives  64.6 us (33%)
  starting transfers between devices  64.5 us (33%)
  waiting for transfers between devices  33.4 us (17%)
  Pallas kernels  24.1 us (12%)
  local copies, waits for them, and re-layouts  2.1 us (1%)
    all_to_all x1, blocking collectives, gathered(): mixed = lax.all_to_all(chunks, 'col', 0, 0, tiled=True)  64.6 us
    ppermute x7, starting transfers between devices, hop(): hops[way].append(lax.ppermute(hops[way][-1], 'row', perm))  21.6 us
    ppermute x7, waiting for transfers between devices, hop(): hops[way].append(lax.ppermute(hops[way][-1], 'row', perm))  20.9 us
    pallas_call x8, Pallas kernels, strips(): pl.pallas_call(functools.partial(strip_kernel, scale, frames, offset), ou...  18.4 us
    all_to_all x1, starting transfers between devices, gathered(): got = lax.all_to_all(routed, 'row', 0, 0, tiled=True)  14.4 us
    ppermute x2, starting transfers between devices, gathered(): b = lax.ppermute(b, 'col', ring_left)  9.19 us
    ppermute x1, waiting for transfers between devices, gathered(): a = lax.ppermute(packed, 'col', ring_right)  8.17 us
    ppermute x1, starting transfers between devices, gathered(): other = lax.ppermute(mine, 'row', swap)  6.05 us
  transfers between devices with their start and end apart: 16, of which 8 were waited for; matrix products, arithmetic and copies ran while one was open for 0% of the time, Pallas kernels for 10%

profile of v3, /device:TPU:65, one launch (start us, length us, event | category | flops | bytes accessed | tf_op | source)
XLA Modules:
  0.0 189.6 jit_solution(3568961677588722956)
XLA Ops:
  2.0 64.6 %all_to_all.10.chunks_ref = bf16[16,16,896]{2,1,0:T(8,128)(2,1)S(1)} all-to-all(bf16[16,16,896]{2,1,0:T(8,128)(2,1)S(1)} %get-tuple-element.15), channel_id=1, replica_groups=mesh['subj'=2,'row'=16,'col'=16] {'col'}, dimensions={0} | all-to-all | bytes 917504 | tf_op jit(solution)/shard_map/all_to_all | solution.py:251
  68.3 14.4 %all-to-all-start.1 = ((bf16[16,16,896]{2,1,0:T(8,128)(2,1)}), bf16[16,16,896]{2,1,0:T(8,128)(2,1)S(1)}, u32[]{:S(2)}, u32[]{:S(2)}) async-start(bf16[16,16,896]{2,1,0:T(8,128)(2,1)} %route.1), calls=%async_computation.1 | async-start | bytes 917504 | tf_op jit(solution)/shard_map/all_to_all | solution.py:269
  82.8 3.3 %collective-permute-start.2 = (bf16[800,128]{1,0:T(8,128)(2,1)S(1)}, bf16[800,128]{1,0:T(8,128)(2,1)S(1)}, u32[]{:S(2)}, u32[]{:S(2)}) collective-permute-start(bf16[800,128]{1,0:T(8,128)(2,1)S(1)} %get-tuple-element.17.refs_0_), channel_id=1, source_target_pairs={{0,32},{16,48},{32,64},{48,80},{64,96},{80,112},{96,128},{112,144}... | collective-permute-start | bytes 614408 | tf_op jit(solution)/shard_map/ppermute | solution.py:255
  86.1 3.3 %collective-permute-start.5 = (bf16[800,128]{1,0:T(8,128)(2,1)S(1)}, bf16[800,128]{1,0:T(8,128)(2,1)S(1)}, u32[]{:S(2)}, u32[]{:S(2)}) collective-permute-start(bf16[800,128]{1,0:T(8,128)(2,1)S(1)} %get-tuple-element.17.refs_0_), channel_id=1, source_target_pairs={{0,224},{16,240},{32,0},{48,16},{64,32},{80,48},{96,64},{112,80},{... | collective-permute-start | bytes 614408 | tf_op jit(solution)/shard_map/ppermute | solution.py:255
  89.3 11.1 %collective-permute-done.2.refs_1_ = bf16[800,128]{1,0:T(8,128)(2,1)S(1)} collective-permute-done((bf16[800,128]{1,0:T(8,128)(2,1)S(1)}, bf16[800,128]{1,0:T(8,128)(2,1)S(1)}, u32[]{:S(2)}, u32[]{:S(2)}) %collective-permute-start.2) | collective-permute-done | bytes 204832 | tf_op jit(solution)/shard_map/ppermute | solution.py:255
  102.4 4.6 %collective-permute-start.6 = (bf16[800,128]{1,0:T(8,128)(2,1)S(1)}, bf16[800,128]{1,0:T(8,128)(2,1)S(1)}, u32[]{:S(2)}, u32[]{:S(2)}) collective-permute-start(bf16[800,128]{1,0:T(8,128)(2,1)S(1)} %collective-permute-done.5.refs_5_), channel_id=1, source_target_pairs={{0,224},{16,240},{32,0},{48,16},{64,32},{80,48},{96,64},{112,80},{... | collective-permute-start | bytes 614408 | tf_op jit(solution)/shard_map/ppermute | solution.py:255
  107.0 2.2 %collective-permute-done.3.refs_2_ = bf16[800,128]{1,0:T(8,128)(2,1)S(1)} collective-permute-done((bf16[800,128]{1,0:T(8,128)(2,1)S(1)}, bf16[800,128]{1,0:T(8,128)(2,1)S(1)}, u32[]{:S(2)}, u32[]{:S(2)}) %collective-permute-start.3) | collective-permute-done | bytes 204832 | tf_op jit(solution)/shard_map/ppermute | solution.py:255
  112.1 4.9 %collective-permute-done.4.refs_3_ = bf16[800,128]{1,0:T(8,128)(2,1)S(1)} collective-permute-done((bf16[800,128]{1,0:T(8,128)(2,1)S(1)}, bf16[800,128]{1,0:T(8,128)(2,1)S(1)}, u32[]{:S(2)}, u32[]{:S(2)}) %collective-permute-start.4) | collective-permute-done | bytes 204832 | tf_op jit(solution)/shard_map/ppermute | solution.py:255
  118.9 4.6 %collective-permute-start.8 = (bf16[800,128]{1,0:T(8,128)(2,1)S(1)}, bf16[800,128]{1,0:T(8,128)(2,1)S(1)}, u32[]{:S(2)}, u32[]{:S(2)}) collective-permute-start(bf16[800,128]{1,0:T(8,128)(2,1)S(1)} %collective-permute-done.6.refs_6_), channel_id=1, source_target_pairs={{0,224},{16,240},{32,0},{48,16},{64,32},{80,48},{96,64},{112,80},{... | collective-permute-start | bytes 614408 | tf_op jit(solution)/shard_map/ppermute | solution.py:255
  126.3 6.0 %collective-permute-start.9 = (bf16[8,800,128]{2,1,0:T(8,128)(2,1)S(1)}, bf16[8,800,128]{2,1,0:T(8,128)(2,1)S(1)}, u32[]{:S(2)}, u32[]{:S(2)}) collective-permute-start(bf16[8,800,128]{2,1,0:T(8,128)(2,1)S(1)} %stack.1.mine_ref), channel_id=1, source_target_pairs={{0,16},{16,0},{32,48},{48,32},{64,80},{80,64},{96,112},{112,96},{1... | collective-permute-start | bytes 4915208 | tf_op jit(solution)/shard_map/ppermute | solution.py:310
  132.3 2.0 %collective-permute-start = (bf16[1600,128]{1,0:T(8,128)(2,1)}, bf16[1600,128]{1,0:T(8,128)(2,1)}, u32[]{:S(2)}, u32[]{:S(2)}) collective-permute-start(bf16[1600,128]{1,0:T(8,128)(2,1)} %pack.1.part), channel_id=1, source_target_pairs={{0,1},{1,2},{2,3},{3,4},{4,5},{5,6},{6,7},{7,8},{8,9},{9,10},{10,1... | collective-permute-start | bytes 1228808 | tf_op jit(solution)/shard_map/ppermute | solution.py:282
  134.3 5.5 %collective-permute-start.11 = (bf16[1600,128]{1,0:T(8,128)(2,1)}, bf16[1600,128]{1,0:T(8,128)(2,1)}, u32[]{:S(2)}, u32[]{:S(2)}) collective-permute-start(bf16[1600,128]{1,0:T(8,128)(2,1)} %pack.1.part), channel_id=1, source_target_pairs={{0,15},{1,0},{2,1},{3,2},{4,3},{5,4},{6,5},{7,6},{8,7},{9,8},{10,9... | collective-permute-start | bytes 1228808 | tf_op jit(solution)/shard_map/ppermute | solution.py:283
  139.8 8.2 %collective-permute-done.part = bf16[1600,128]{1,0:T(8,128)(2,1)} collective-permute-done((bf16[1600,128]{1,0:T(8,128)(2,1)}, bf16[1600,128]{1,0:T(8,128)(2,1)}, u32[]{:S(2)}, u32[]{:S(2)}) %collective-permute-start) | collective-permute-done | bytes 409632 | tf_op jit(solution)/shard_map/ppermute | solution.py:282
  152.0 4.6 %collective-permute-start.12 = (bf16[1600,128]{1,0:T(8,128)(2,1)}, bf16[1600,128]{1,0:T(8,128)(2,1)S(1)}, u32[]{:S(2)}, u32[]{:S(2)}) collective-permute-start(bf16[1600,128]{1,0:T(8,128)(2,1)} %collective-permute-done.11.part), channel_id=1, source_target_pairs={{0,15},{1,0},{2,1},{3,2},{4,3},{5,4},{6,5},{7,6},{8,7},{9,8},{10,9... | collective-permute-start | bytes 1228808 | tf_op jit(solution)/shard_map/ppermute | solution.py:328
  156.6 2.4 %strips.8._ = bf16[96,128,128]{2,1,0:T(8,128)(2,1)S(1)} custom-call(s32[8,128]{1,0:T(8,128)S(1)} %get-tuple-element.16.code_ref, bf16[1600,128]{1,0:T(8,128)(2,1)} %pack.1.part, bf16[8,800,128]{2,1,0:T(8,128)(2,1)S(1)} %stack.1.mine_ref, bf16[8,800,128]{2,1,0:T(8,128)(2,1)S(1)} %collective-permute-done.9.other_ref, ...), custom_call_target="tpu_custom_call", output_to_operand_aliasing={{}: (4, {})} | custom-call | tf_op jit(solution)/shard_map/strips/pallas_call | solution.py:183
  159.0 2.9 %collective-permute-done.1.part = bf16[1600,128]{1,0:T(8,128)(2,1)} collective-permute-done((bf16[1600,128]{1,0:T(8,128)(2,1)}, bf16[1600,128]{1,0:T(8,128)(2,1)}, u32[]{:S(2)}, u32[]{:S(2)}) %collective-permute-start.1) | collective-permute-done | bytes 409632 | tf_op jit(solution)/shard_map/ppermute | solution.py:322
  163.8 2.4 %strips.9._ = bf16[96,128,128]{2,1,0:T(8,128)(2,1)S(1)} custom-call(s32[8,128]{1,0:T(8,128)S(1)} %get-tuple-element.16.code_ref, bf16[1600,128]{1,0:T(8,128)(2,1)} %collective-permute-done.part, bf16[8,800,128]{2,1,0:T(8,128)(2,1)S(1)} %stack.1.mine_ref, bf16[8,800,128]{2,1,0:T(8,128)(2,1)S(1)} %collective-permute-done.9.other_ref, ...), custom_call_target="tpu_custom_call", output_to_operand_aliasing={{}: (4, {})} | custom-call | tf_op jit(solution)/shard_map/strips/pallas_call | solution.py:183
  166.2 4.6 %collective-permute-start.14 = (bf16[1600,128]{1,0:T(8,128)(2,1)S(1)}, bf16[1600,128]{1,0:T(8,128)(2,1)S(1)}, u32[]{:S(2)}, u32[]{:S(2)}) collective-permute-start(bf16[1600,128]{1,0:T(8,128)(2,1)S(1)} %collective-permute-done.12.part), channel_id=1, source_target_pairs={{0,15},{1,0},{2,1},{3,2},{4,3},{5,4},{6,5},{7,6},{8,7},{9,8},{10,9... | collective-permute-start | bytes 1228808 | tf_op jit(solution)/shard_map/ppermute | solution.py:328
  170.8 2.4 %strips.10._ = bf16[96,128,128]{2,1,0:T(8,128)(2,1)S(1)} custom-call(s32[8,128]{1,0:T(8,128)S(1)} %get-tuple-element.16.code_ref, bf16[1600,128]{1,0:T(8,128)(2,1)} %collective-permute-done.11.part, bf16[8,800,128]{2,1,0:T(8,128)(2,1)S(1)} %stack.1.mine_ref, ...), custom_call_target="tpu_custom_call", output_to_operand_aliasing={{}: (4, {})} | custom-call | tf_op jit(solution)/shard_map/strips/pallas_call | solution.py:183
  176.7 2.4 %strips.11._ = bf16[96,128,128]{2,1,0:T(8,128)(2,1)S(1)} custom-call(s32[8,128]{1,0:T(8,128)S(1)} %get-tuple-element.16.code_ref, bf16[1600,128]{1,0:T(8,128)(2,1)} %collective-permute-done.1.part, bf16[8,800,128]{2,1,0:T(8,128)(2,1)S(1)} %stack.1.mine_ref, ...), custom_call_target="tpu_custom_call", output_to_operand_aliasing={{}: (4, {})} | custom-call | tf_op jit(solution)/shard_map/strips/pallas_call | solution.py:183
  179.1 2.0 %strips.12._ = bf16[96,128,128]{2,1,0:T(8,128)(2,1)S(1)} custom-call(s32[8,128]{1,0:T(8,128)S(1)} %get-tuple-element.16.code_ref, bf16[1600,128]{1,0:T(8,128)(2,1)S(1)} %collective-permute-done.12.part, bf16[8,800,128]{2,1,0:T(8,128)(2,1)S(1)} %stack.1.mine_ref, ...), custom_call_target="tpu_custom_call", output_to_operand_aliasing={{}: (4, {})} | custom-call | tf_op jit(solution)/shard_map/strips/pallas_call | solution.py:183
  181.1 2.0 %strips.13._ = bf16[96,128,128]{2,1,0:T(8,128)(2,1)S(1)} custom-call(s32[8,128]{1,0:T(8,128)S(1)} %get-tuple-element.16.code_ref, bf16[1600,128]{1,0:T(8,128)(2,1)S(1)} %collective-permute-done.10.part, bf16[8,800,128]{2,1,0:T(8,128)(2,1)S(1)} %stack.1.mine_ref, ...), custom_call_target="tpu_custom_call", output_to_operand_aliasing={{}: (4, {})} | custom-call | tf_op jit(solution)/shard_map/strips/pallas_call | solution.py:183
  183.2 2.0 %strips.14.filled_ref = bf16[96,128,128]{2,1,0:T(8,128)(2,1)S(1)} custom-call(s32[8,128]{1,0:T(8,128)S(1)} %get-tuple-element.16.code_ref, bf16[1600,128]{1,0:T(8,128)(2,1)S(1)} %collective-permute-done.14.part, bf16[8,800,128]{2,1,0:T(8,128)(2,1)S(1)} %stack.1.mine_ref, ...), custom_call_target="tpu_custom_call", output_to_operand_aliasing={{}: (4, {})} | custom-call | tf_op jit(solution)/shard_map/strips/pallas_call | solution.py:183
  186.9 2.7 %strips.15 = bf16[96,128,128]{2,1,0:T(8,128)(2,1)} custom-call(s32[8,128]{1,0:T(8,128)S(1)} %get-tuple-element.16.code_ref, bf16[1600,128]{1,0:T(8,128)(2,1)S(1)} %collective-permute-done.13.part, bf16[8,800,128]{2,1,0:T(8,128)(2,1)S(1)} %stack.1.mine_ref, bf16[8,800,128]{2,1,0:T(8,128)(2,1)S(1)} %collective-permute-done.9.other_ref, ...), custom_call_target="tpu_custom_call", output_to_operand_aliasing={{}: (4, {})} | custom-call | tf_op jit(solution)/shard_map/strips/pallas_call | solution.py:183
  (33 shorter events, 23.6 us)
Async XLA Ops:
  0.6 1.0 copy-start.2
  66.6 83.3 %copy-start.3 = (s32[256]{0:T(256)S(1)}, s32[256]{0:T(256)}, u32[]{:S(2)}) copy-start(s32[256]{0:T(256)} %owner_ref.1) | copy-start | bytes 3076
  68.3 42.8 %all-to-all-start.1 = ((bf16[16,16,896]{2,1,0:T(8,128)(2,1)}), bf16[16,16,896]{2,1,0:T(8,128)(2,1)S(1)}, u32[]{:S(2)}, u32[]{:S(2)}) async-start(bf16[16,16,896]{2,1,0:T(8,128)(2,1)} %route.1), calls=%async_computation.1 | async-start | bytes 917504 | tf_op jit(solution)/shard_map/all_to_all | solution.py:269
  82.8 17.7 %collective-permute-start.2 = (bf16[800,128]{1,0:T(8,128)(2,1)S(1)}, bf16[800,128]{1,0:T(8,128)(2,1)S(1)}, u32[]{:S(2)}, u32[]{:S(2)}) collective-permute-start(bf16[800,128]{1,0:T(8,128)(2,1)S(1)} %get-tuple-element.17.refs_0_), channel_id=1, source_target_pairs={{0,32},{16,48},{32,64},{48,80},{64,96},{80,112},{96,128},{112,144}... | collective-permute-start | bytes 614408 | tf_op jit(solution)/shard_map/ppermute | solution.py:255
  86.1 16.3 %collective-permute-start.5 = (bf16[800,128]{1,0:T(8,128)(2,1)S(1)}, bf16[800,128]{1,0:T(8,128)(2,1)S(1)}, u32[]{:S(2)}, u32[]{:S(2)}) collective-permute-start(bf16[800,128]{1,0:T(8,128)(2,1)S(1)} %get-tuple-element.17.refs_0_), channel_id=1, source_target_pairs={{0,224},{16,240},{32,0},{48,16},{64,32},{80,48},{96,64},{112,80},{... | collective-permute-start | bytes 614408 | tf_op jit(solution)/shard_map/ppermute | solution.py:255
  100.4 8.8 %collective-permute-start.3 = (bf16[800,128]{1,0:T(8,128)(2,1)S(1)}, bf16[800,128]{1,0:T(8,128)(2,1)S(1)}, u32[]{:S(2)}, u32[]{:S(2)}) collective-permute-start(bf16[800,128]{1,0:T(8,128)(2,1)S(1)} %collective-permute-done.2.refs_1_), channel_id=1, source_target_pairs={{0,32},{16,48},{32,64},{48,80},{64,96},{80,112},{96,128},{112,144}... | collective-permute-start | bytes 614408 | tf_op jit(solution)/shard_map/ppermute | solution.py:255
  102.4 9.7 %collective-permute-start.6 = (bf16[800,128]{1,0:T(8,128)(2,1)S(1)}, bf16[800,128]{1,0:T(8,128)(2,1)S(1)}, u32[]{:S(2)}, u32[]{:S(2)}) collective-permute-start(bf16[800,128]{1,0:T(8,128)(2,1)S(1)} %collective-permute-done.5.refs_5_), channel_id=1, source_target_pairs={{0,224},{16,240},{32,0},{48,16},{64,32},{80,48},{96,64},{112,80},{... | collective-permute-start | bytes 614408 | tf_op jit(solution)/shard_map/ppermute | solution.py:255
  109.2 7.7 %collective-permute-start.4 = (bf16[800,128]{1,0:T(8,128)(2,1)S(1)}, bf16[800,128]{1,0:T(8,128)(2,1)S(1)}, u32[]{:S(2)}, u32[]{:S(2)}) collective-permute-start(bf16[800,128]{1,0:T(8,128)(2,1)S(1)} %collective-permute-done.3.refs_2_), channel_id=1, source_target_pairs={{0,32},{16,48},{32,64},{48,80},{64,96},{80,112},{96,128},{112,144}... | collective-permute-start | bytes 614408 | tf_op jit(solution)/shard_map/ppermute | solution.py:255
  111.2 13.5 %copy-start = (bf16[16,16,896]{2,1,0:T(8,128)(2,1)}, bf16[16,16,896]{2,1,0:T(8,128)(2,1)S(1)}, u32[]{:S(2)}) copy-start(bf16[16,16,896]{2,1,0:T(8,128)(2,1)S(1)} %all-to-all-done.1.got_ref) | copy-start | bytes 1376260
  116.9 7.7 %collective-permute-start.7 = (bf16[800,128]{1,0:T(8,128)(2,1)S(1)}, bf16[800,128]{1,0:T(8,128)(2,1)S(1)}, u32[]{:S(2)}, u32[]{:S(2)}) collective-permute-start(bf16[800,128]{1,0:T(8,128)(2,1)S(1)} %collective-permute-done.4.refs_3_), channel_id=1, source_target_pairs={{0,32},{16,48},{32,64},{48,80},{64,96},{80,112},{96,128},{112,144}... | collective-permute-start | bytes 614408 | tf_op jit(solution)/shard_map/ppermute | solution.py:255
  118.9 7.3 %collective-permute-start.8 = (bf16[800,128]{1,0:T(8,128)(2,1)S(1)}, bf16[800,128]{1,0:T(8,128)(2,1)S(1)}, u32[]{:S(2)}, u32[]{:S(2)}) collective-permute-start(bf16[800,128]{1,0:T(8,128)(2,1)S(1)} %collective-permute-done.6.refs_6_), channel_id=1, source_target_pairs={{0,224},{16,240},{32,0},{48,16},{64,32},{80,48},{96,64},{112,80},{... | collective-permute-start | bytes 614408 | tf_op jit(solution)/shard_map/ppermute | solution.py:255
  126.3 30.3 %collective-permute-start.9 = (bf16[8,800,128]{2,1,0:T(8,128)(2,1)S(1)}, bf16[8,800,128]{2,1,0:T(8,128)(2,1)S(1)}, u32[]{:S(2)}, u32[]{:S(2)}) collective-permute-start(bf16[8,800,128]{2,1,0:T(8,128)(2,1)S(1)} %stack.1.mine_ref), channel_id=1, source_target_pairs={{0,16},{16,0},{32,48},{48,32},{64,80},{80,64},{96,112},{112,96},{1... | collective-permute-start | bytes 4915208 | tf_op jit(solution)/shard_map/ppermute | solution.py:310
  132.3 15.6 %collective-permute-start = (bf16[1600,128]{1,0:T(8,128)(2,1)}, bf16[1600,128]{1,0:T(8,128)(2,1)}, u32[]{:S(2)}, u32[]{:S(2)}) collective-permute-start(bf16[1600,128]{1,0:T(8,128)(2,1)} %pack.1.part), channel_id=1, source_target_pairs={{0,1},{1,2},{2,3},{3,4},{4,5},{5,6},{6,7},{7,8},{8,9},{9,10},{10,1... | collective-permute-start | bytes 1228808 | tf_op jit(solution)/shard_map/ppermute | solution.py:282
  134.3 17.6 %collective-permute-start.11 = (bf16[1600,128]{1,0:T(8,128)(2,1)}, bf16[1600,128]{1,0:T(8,128)(2,1)}, u32[]{:S(2)}, u32[]{:S(2)}) collective-permute-start(bf16[1600,128]{1,0:T(8,128)(2,1)} %pack.1.part), channel_id=1, source_target_pairs={{0,15},{1,0},{2,1},{3,2},{4,3},{5,4},{6,5},{7,6},{8,7},{9,8},{10,9... | collective-permute-start | bytes 1228808 | tf_op jit(solution)/shard_map/ppermute | solution.py:283
  148.0 13.9 %collective-permute-start.1 = (bf16[1600,128]{1,0:T(8,128)(2,1)}, bf16[1600,128]{1,0:T(8,128)(2,1)}, u32[]{:S(2)}, u32[]{:S(2)}) collective-permute-start(bf16[1600,128]{1,0:T(8,128)(2,1)} %collective-permute-done.part), channel_id=1, source_target_pairs={{0,1},{1,2},{2,3},{3,4},{4,5},{5,6},{6,7},{7,8},{8,9},{9,10},{10,1... | collective-permute-start | bytes 1228808 | tf_op jit(solution)/shard_map/ppermute | solution.py:322
  150.0 1.0 copy-start.1
  152.0 14.3 %collective-permute-start.12 = (bf16[1600,128]{1,0:T(8,128)(2,1)}, bf16[1600,128]{1,0:T(8,128)(2,1)S(1)}, u32[]{:S(2)}, u32[]{:S(2)}) collective-permute-start(bf16[1600,128]{1,0:T(8,128)(2,1)} %collective-permute-done.11.part), channel_id=1, source_target_pairs={{0,15},{1,0},{2,1},{3,2},{4,3},{5,4},{6,5},{7,6},{8,7},{9,8},{10,9... | collective-permute-start | bytes 1228808 | tf_op jit(solution)/shard_map/ppermute | solution.py:328
  161.8 12.9 %collective-permute-start.10 = (bf16[1600,128]{1,0:T(8,128)(2,1)}, bf16[1600,128]{1,0:T(8,128)(2,1)S(1)}, u32[]{:S(2)}, u32[]{:S(2)}) collective-permute-start(bf16[1600,128]{1,0:T(8,128)(2,1)} %collective-permute-done.1.part), channel_id=1, source_target_pairs={{0,1},{1,2},{2,3},{3,4},{4,5},{5,6},{6,7},{7,8},{8,9},{9,10},{10,1... | collective-permute-start | bytes 1228808 | tf_op jit(solution)/shard_map/ppermute | solution.py:322
  166.2 16.9 %collective-permute-start.14 = (bf16[1600,128]{1,0:T(8,128)(2,1)S(1)}, bf16[1600,128]{1,0:T(8,128)(2,1)S(1)}, u32[]{:S(2)}, u32[]{:S(2)}) collective-permute-start(bf16[1600,128]{1,0:T(8,128)(2,1)S(1)} %collective-permute-done.12.part), channel_id=1, source_target_pairs={{0,15},{1,0},{2,1},{3,2},{4,3},{5,4},{6,5},{7,6},{8,7},{9,8},{10,9... | collective-permute-start | bytes 1228808 | tf_op jit(solution)/shard_map/ppermute | solution.py:328
  174.8 12.1 %collective-permute-start.13 = (bf16[1600,128]{1,0:T(8,128)(2,1)S(1)}, bf16[1600,128]{1,0:T(8,128)(2,1)S(1)}, u32[]{:S(2)}, u32[]{:S(2)}) collective-permute-start(bf16[1600,128]{1,0:T(8,128)(2,1)S(1)} %collective-permute-done.10.part), channel_id=1, source_target_pairs={{0,1},{1,2},{2,3},{3,4},{4,5},{5,6},{6,7},{7,8},{8,9},{9,10},{10,1... | collective-permute-start | bytes 1228808 | tf_op jit(solution)/shard_map/ppermute | solution.py:322

commit v4 on v3

--- a/solution.py
+++ b/solution.py
@@ -20,72 +20,74 @@
 
 def score_kernel(series_ref, scored_ref, chunks_ref):
     frames = series_ref.shape[0]
-    _, sub, padded = chunks_ref.shape
-    groups = LANES // sub
+    groups = chunks_ref.shape[0] // COPIES
+    sub = LANES // groups
+    blocks = frames // LANES
+    gap = frames - blocks * LANES
+    per = LANES // gap
     x = series_ref[...]
     centred = x - jnp.sum(x, axis=0, keepdims=True) * (1.0 / frames)
     spread = jnp.sum(centred * centred, axis=0, keepdims=True) * (1.0 / frames)
     z = centred * lax.rsqrt(spread + EPS)
     scored_ref[...] = z.astype(jnp.bfloat16)
-    for b in range(padded // LANES):
-        rows = min(LANES, frames - b * LANES)
-        part = z[b * LANES : b * LANES + rows]
-        if rows < LANES:
-            part = jnp.concatenate([part, jnp.zeros((LANES - rows, LANES), jnp.float32)], axis=0)
-        flipped = part.T.astype(jnp.bfloat16)
+    for b in range(blocks):
+        flipped = z[b * LANES : (b + 1) * LANES].T.astype(jnp.bfloat16)
         flipped = flipped.reshape(groups, sub, LANES)
         for copy in range(COPIES):
             at = copy * groups
-            chunks_ref[at : at + groups, :, b * LANES : (b + 1) * LANES] = flipped
-
-
-def route_kernel(frames, owner_ref, chunks_ref, keep_ref, out_ref):
-    n = chunks_ref.shape[0]
-    padded = chunks_ref.shape[2]
-    last = padded - LANES
-    gap = frames - last
+            chunks_ref[at : at + groups, b * sub : (b + 1) * sub, :] = flipped
+    tail = jnp.concatenate([z[blocks * LANES :], jnp.zeros((LANES - gap, LANES), jnp.float32)])
+    tail = tail.T.reshape(groups, sub, LANES)
+    few = sub // per
+    tail = jnp.concatenate([tail[:, q * few : (q + 1) * few, :gap] for q in range(per)], axis=2)
+    spare = chunks_ref.shape[1] - blocks * sub
+    tail = jnp.concatenate(
+        [tail, jnp.zeros((groups, spare - few, LANES), jnp.float32)], axis=1
+    ).astype(jnp.bfloat16)
+    for copy in range(COPIES):
+        at = copy * groups
+        chunks_ref[at : at + groups, blocks * sub :, :] = tail
+
+
+def route_kernel(spare, owner_ref, chunks_ref, keep_ref, out_ref):
+    n, height, _ = chunks_ref.shape
+    last = height - ALIGN
     flags = keep_ref[...].astype(jnp.float32)
-    flags = jnp.concatenate(
-        [
-            jnp.zeros((n, gap), jnp.float32),
-            flags,
-            jnp.zeros((n, LANES - gap - flags.shape[1]), jnp.float32),
-        ],
-        axis=1,
-    )
+    flags = jnp.concatenate([flags, jnp.zeros((n, LANES - flags.shape[1]), jnp.float32)], axis=1)
+    at_spare = lax.broadcasted_iota(jnp.int32, (ALIGN, LANES), 0) >= ALIGN - spare
     base = lax.axis_index("row") * n
     for k in range(n):
         owner = owner_ref[base + k]
-        out_ref[owner, :, :last] = chunks_ref[k, :, :last]
-        tail = chunks_ref[k, :, last:].astype(jnp.float32) + flags[k : k + 1]
-        out_ref[owner, :, last:] = tail.astype(jnp.bfloat16)
+        out_ref[owner, :last, :] = chunks_ref[k, :last, :]
+        tail = jnp.where(at_spare, flags[k : k + 1], chunks_ref[k, last:, :].astype(jnp.float32))
+        out_ref[owner, last:, :] = tail.astype(jnp.bfloat16)
 
 
 def pack_kernel(frames, got_ref, packed_ref):
-    n, sub, padded = got_ref.shape
-    rows = n * sub
-    last = padded - LANES
-    gap = frames - last
-    blocks = [
-        got_ref[:, :, b : b + LANES].reshape(rows, LANES) for b in range(0, last, LANES)
-    ]
-    tail = got_ref[:, :, last:].reshape(rows, LANES)
+    n = got_ref.shape[0]
+    blocks = frames // LANES
+    gap = frames - blocks * LANES
+    rows = packed_ref.shape[0] * LANES // frames
+    sub = rows // n
+    for b in range(blocks):
+        block = got_ref[:, b * sub : (b + 1) * sub, :]
+        packed_ref[b * rows : (b + 1) * rows, :] = block.reshape(rows, LANES)
     per = LANES // gap
+    few = sub // per
+    tail = got_ref[:, blocks * sub :, :].astype(jnp.float32)[:, :few]
+    tail = jnp.concatenate([tail[:, :, q * gap : (q + 1) * gap] for q in range(per)], axis=1)
+    tail = tail.reshape(rows, gap)
     depth = rows // per
-    tail = jnp.concatenate([tail[q * depth : (q + 1) * depth, :gap] for q in range(per)], axis=1)
-    for b, block in enumerate(blocks):
-        packed_ref[b * rows : (b + 1) * rows, :] = block
-    packed_ref[len(blocks) * rows :, :] = tail
-
-
-def list_kernel(frames, got_ref, owner_ref, code_ref, ids_ref):
-    n, sub, padded = got_ref.shape
-    rows = n * sub
-    last = padded - LANES
-    gap = frames - last
+    tail = jnp.concatenate([tail[q * depth : (q + 1) * depth] for q in range(per)], axis=1)
+    packed_ref[blocks * rows :, :] = tail.astype(jnp.bfloat16)
+
+
+def list_kernel(rows, got_ref, owner_ref, code_ref, ids_ref):
+    n, height, _ = got_ref.shape
+    sub = rows // n
     me = lax.axis_index("row")
     block = lax.axis_index("col")
-    flags = got_ref[:, 0, last:].astype(jnp.float32)[:, gap : gap + n]
+    flags = got_ref[:, height - ALIGN :, :].astype(jnp.float32)[:, ALIGN - 1, :n]
     r_of = lax.broadcasted_iota(jnp.int32, (n, n), 0)
     k_of = lax.broadcasted_iota(jnp.int32, (n, n), 1)
     upper = (r_of <= k_of).astype(jnp.float32)
@@ -228,16 +230,17 @@
     row_count, col_count = keep_mask.shape
     slot_limit = max(2, 3 * col_count // 8)
     capacity = row_count * slot_limit
-    padded = -(-frames // LANES) * LANES
     groups = n_col // COPIES
     sub = LANES // groups
+    used = frames * sub // LANES
+    height = (used // ALIGN + 1) * ALIGN
     bf16 = jnp.bfloat16
     sds = jax.ShapeDtypeStruct
 
     small = pltpu.CompilerParams(vmem_limit_bytes=VMEM_LIMIT)
     scored, chunks = pl.pallas_call(
         score_kernel,
-        out_shape=(pltpu.VMEM((frames, LANES), bf16), pltpu.VMEM((n_col, sub, padded), bf16)),
+        out_shape=(pltpu.VMEM((frames, LANES), bf16), pltpu.VMEM((n_col, height, LANES), bf16)),
         in_specs=[VMEM],
         out_specs=(VMEM, VMEM),
         compiler_params=small,
@@ -259,8 +262,8 @@
         if step < chips // 2 - 1:
             hop("left", left)
     routed = pl.pallas_call(
-        functools.partial(route_kernel, frames),
-        out_shape=pltpu.VMEM((n_row, sub, padded), bf16),
+        functools.partial(route_kernel, height - used),
+        out_shape=pltpu.VMEM((n_row, height, LANES), bf16),
         in_specs=[SMEM, VMEM, VMEM],
         out_specs=VMEM,
         compiler_params=small,
@@ -283,7 +286,7 @@
     b = lax.ppermute(packed, "col", ring_left)
 
     code, ids = pl.pallas_call(
-        functools.partial(list_kernel, frames),
+        functools.partial(list_kernel, n_row * sub),
         out_shape=(
             sds((ALIGN, LANES), jnp.int32),
             sds((1, 1, capacity), jnp.int32),

time: 193 us -> 191 us (0.990)
  no operation moved by 1% of the time
where the time goes in v4:
time: 191 us; the launch traced here: 187 us
  blocking collectives  64 us (34%)
  starting transfers between devices  63.4 us (33%)
  waiting for transfers between devices  32.8 us (17%)
  Pallas kernels  23.9 us (13%)
  local copies, waits for them, and re-layouts  2.1 us (1%)
    all_to_all x1, blocking collectives, gathered(): mixed = lax.all_to_all(chunks, 'col', 0, 0, tiled=True)  64 us
    ppermute x7, starting transfers between devices, hop(): hops[way].append(lax.ppermute(hops[way][-1], 'row', perm))  21.6 us
    ppermute x7, waiting for transfers between devices, hop(): hops[way].append(lax.ppermute(hops[way][-1], 'row', perm))  20.1 us
    pallas_call x8, Pallas kernels, strips(): pl.pallas_call(functools.partial(strip_kernel, scale, frames, offset), ou...  18.4 us
    all_to_all x1, starting transfers between devices, gathered(): got = lax.all_to_all(routed, 'row', 0, 0, tiled=True)  13.3 us
    ppermute x2, starting transfers between devices, gathered(): b = lax.ppermute(b, 'col', ring_left)  9.19 us
    ppermute x1, waiting for transfers between devices, gathered(): a = lax.ppermute(packed, 'col', ring_right)  8.17 us
    ppermute x1, starting transfers between devices, gathered(): other = lax.ppermute(mine, 'row', swap)  6.05 us
  transfers between devices with their start and end apart: 16, of which 8 were waited for; matrix products, arithmetic and copies ran while one was open for 0% of the time, Pallas kernels for 10%

profile of v4, /device:TPU:65, one launch (start us, length us, event | category | flops | bytes accessed | tf_op | source)
XLA Modules:
  0.0 187.1 jit_solution(11537473655877268153)
XLA Ops:
  2.1 64.0 %all_to_all.10.chunks_ref = bf16[16,104,128]{2,1,0:T(8,128)(2,1)S(1)} all-to-all(bf16[16,104,128]{2,1,0:T(8,128)(2,1)S(1)} %get-tuple-element.15), channel_id=1, replica_groups=mesh['subj'=2,'row'=16,'col'=16] {'col'}, dimensions={0} | all-to-all | bytes 851968 | tf_op jit(solution)/shard_map/all_to_all | solution.py:254
  67.5 13.3 %all-to-all-start.1 = ((bf16[16,104,128]{2,1,0:T(8,128)(2,1)}), bf16[16,104,128]{2,1,0:T(8,128)(2,1)S(1)}, u32[]{:S(2)}, u32[]{:S(2)}) async-start(bf16[16,104,128]{2,1,0:T(8,128)(2,1)} %route.1), calls=%async_computation.1 | async-start | bytes 851968 | tf_op jit(solution)/shard_map/all_to_all | solution.py:272
  80.9 3.3 %collective-permute-start.2 = (bf16[800,128]{1,0:T(8,128)(2,1)S(1)}, bf16[800,128]{1,0:T(8,128)(2,1)S(1)}, u32[]{:S(2)}, u32[]{:S(2)}) collective-permute-start(bf16[800,128]{1,0:T(8,128)(2,1)S(1)} %get-tuple-element.17.refs_0_), channel_id=1, source_target_pairs={{0,32},{16,48},{32,64},{48,80},{64,96},{80,112},{96,128},{112,144}... | collective-permute-start | bytes 614408 | tf_op jit(solution)/shard_map/ppermute | solution.py:258
  84.2 3.3 %collective-permute-start.5 = (bf16[800,128]{1,0:T(8,128)(2,1)S(1)}, bf16[800,128]{1,0:T(8,128)(2,1)S(1)}, u32[]{:S(2)}, u32[]{:S(2)}) collective-permute-start(bf16[800,128]{1,0:T(8,128)(2,1)S(1)} %get-tuple-element.17.refs_0_), channel_id=1, source_target_pairs={{0,224},{16,240},{32,0},{48,16},{64,32},{80,48},{96,64},{112,80},{... | collective-permute-start | bytes 614408 | tf_op jit(solution)/shard_map/ppermute | solution.py:258
  87.4 10.4 %collective-permute-done.2.refs_1_ = bf16[800,128]{1,0:T(8,128)(2,1)S(1)} collective-permute-done((bf16[800,128]{1,0:T(8,128)(2,1)S(1)}, bf16[800,128]{1,0:T(8,128)(2,1)S(1)}, u32[]{:S(2)}, u32[]{:S(2)}) %collective-permute-start.2) | collective-permute-done | bytes 204832 | tf_op jit(solution)/shard_map/ppermute | solution.py:258
  99.8 4.6 %collective-permute-start.6 = (bf16[800,128]{1,0:T(8,128)(2,1)S(1)}, bf16[800,128]{1,0:T(8,128)(2,1)S(1)}, u32[]{:S(2)}, u32[]{:S(2)}) collective-permute-start(bf16[800,128]{1,0:T(8,128)(2,1)S(1)} %collective-permute-done.5.refs_5_), channel_id=1, source_target_pairs={{0,224},{16,240},{32,0},{48,16},{64,32},{80,48},{96,64},{112,80},{... | collective-permute-start | bytes 614408 | tf_op jit(solution)/shard_map/ppermute | solution.py:258
  104.4 2.2 %collective-permute-done.3.refs_2_ = bf16[800,128]{1,0:T(8,128)(2,1)S(1)} collective-permute-done((bf16[800,128]{1,0:T(8,128)(2,1)S(1)}, bf16[800,128]{1,0:T(8,128)(2,1)S(1)}, u32[]{:S(2)}, u32[]{:S(2)}) %collective-permute-start.3) | collective-permute-done | bytes 204832 | tf_op jit(solution)/shard_map/ppermute | solution.py:258
  109.5 4.8 %collective-permute-done.4.refs_3_ = bf16[800,128]{1,0:T(8,128)(2,1)S(1)} collective-permute-done((bf16[800,128]{1,0:T(8,128)(2,1)S(1)}, bf16[800,128]{1,0:T(8,128)(2,1)S(1)}, u32[]{:S(2)}, u32[]{:S(2)}) %collective-permute-start.4) | collective-permute-done | bytes 204832 | tf_op jit(solution)/shard_map/ppermute | solution.py:258
  116.3 4.6 %collective-permute-start.8 = (bf16[800,128]{1,0:T(8,128)(2,1)S(1)}, bf16[800,128]{1,0:T(8,128)(2,1)S(1)}, u32[]{:S(2)}, u32[]{:S(2)}) collective-permute-start(bf16[800,128]{1,0:T(8,128)(2,1)S(1)} %collective-permute-done.6.refs_6_), channel_id=1, source_target_pairs={{0,224},{16,240},{32,0},{48,16},{64,32},{80,48},{96,64},{112,80},{... | collective-permute-start | bytes 614408 | tf_op jit(solution)/shard_map/ppermute | solution.py:258
  123.7 6.0 %collective-permute-start.9 = (bf16[8,800,128]{2,1,0:T(8,128)(2,1)S(1)}, bf16[8,800,128]{2,1,0:T(8,128)(2,1)S(1)}, u32[]{:S(2)}, u32[]{:S(2)}) collective-permute-start(bf16[8,800,128]{2,1,0:T(8,128)(2,1)S(1)} %stack.1.mine_ref), channel_id=1, source_target_pairs={{0,16},{16,0},{32,48},{48,32},{64,80},{80,64},{96,112},{112,96},{1... | collective-permute-start | bytes 4915208 | tf_op jit(solution)/shard_map/ppermute | solution.py:313
  129.8 2.0 %collective-permute-start = (bf16[1600,128]{1,0:T(8,128)(2,1)}, bf16[1600,128]{1,0:T(8,128)(2,1)}, u32[]{:S(2)}, u32[]{:S(2)}) collective-permute-start(bf16[1600,128]{1,0:T(8,128)(2,1)} %pack.1.part), channel_id=1, source_target_pairs={{0,1},{1,2},{2,3},{3,4},{4,5},{5,6},{6,7},{7,8},{8,9},{9,10},{10,1... | collective-permute-start | bytes 1228808 | tf_op jit(solution)/shard_map/ppermute | solution.py:285
  131.7 5.5 %collective-permute-start.11 = (bf16[1600,128]{1,0:T(8,128)(2,1)}, bf16[1600,128]{1,0:T(8,128)(2,1)}, u32[]{:S(2)}, u32[]{:S(2)}) collective-permute-start(bf16[1600,128]{1,0:T(8,128)(2,1)} %pack.1.part), channel_id=1, source_target_pairs={{0,15},{1,0},{2,1},{3,2},{4,3},{5,4},{6,5},{7,6},{8,7},{9,8},{10,9... | collective-permute-start | bytes 1228808 | tf_op jit(solution)/shard_map/ppermute | solution.py:286
  137.3 8.2 %collective-permute-done.part = bf16[1600,128]{1,0:T(8,128)(2,1)} collective-permute-done((bf16[1600,128]{1,0:T(8,128)(2,1)}, bf16[1600,128]{1,0:T(8,128)(2,1)}, u32[]{:S(2)}, u32[]{:S(2)}) %collective-permute-start) | collective-permute-done | bytes 409632 | tf_op jit(solution)/shard_map/ppermute | solution.py:285
  149.3 4.6 %collective-permute-start.12 = (bf16[1600,128]{1,0:T(8,128)(2,1)}, bf16[1600,128]{1,0:T(8,128)(2,1)S(1)}, u32[]{:S(2)}, u32[]{:S(2)}) collective-permute-start(bf16[1600,128]{1,0:T(8,128)(2,1)} %collective-permute-done.11.part), channel_id=1, source_target_pairs={{0,15},{1,0},{2,1},{3,2},{4,3},{5,4},{6,5},{7,6},{8,7},{9,8},{10,9... | collective-permute-start | bytes 1228808 | tf_op jit(solution)/shard_map/ppermute | solution.py:331
  153.9 2.4 %strips.8._ = bf16[96,128,128]{2,1,0:T(8,128)(2,1)S(1)} custom-call(s32[8,128]{1,0:T(8,128)S(1)} %get-tuple-element.16.code_ref, bf16[1600,128]{1,0:T(8,128)(2,1)} %pack.1.part, bf16[8,800,128]{2,1,0:T(8,128)(2,1)S(1)} %stack.1.mine_ref, bf16[8,800,128]{2,1,0:T(8,128)(2,1)S(1)} %collective-permute-done.9.other_ref, ...), custom_call_target="tpu_custom_call", output_to_operand_aliasing={{}: (4, {})} | custom-call | tf_op jit(solution)/shard_map/strips/pallas_call | solution.py:185
  156.4 2.9 %collective-permute-done.1.part = bf16[1600,128]{1,0:T(8,128)(2,1)} collective-permute-done((bf16[1600,128]{1,0:T(8,128)(2,1)}, bf16[1600,128]{1,0:T(8,128)(2,1)}, u32[]{:S(2)}, u32[]{:S(2)}) %collective-permute-start.1) | collective-permute-done | bytes 409632 | tf_op jit(solution)/shard_map/ppermute | solution.py:325
  161.2 2.4 %strips.9._ = bf16[96,128,128]{2,1,0:T(8,128)(2,1)S(1)} custom-call(s32[8,128]{1,0:T(8,128)S(1)} %get-tuple-element.16.code_ref, bf16[1600,128]{1,0:T(8,128)(2,1)} %collective-permute-done.part, bf16[8,800,128]{2,1,0:T(8,128)(2,1)S(1)} %stack.1.mine_ref, bf16[8,800,128]{2,1,0:T(8,128)(2,1)S(1)} %collective-permute-done.9.other_ref, ...), custom_call_target="tpu_custom_call", output_to_operand_aliasing={{}: (4, {})} | custom-call | tf_op jit(solution)/shard_map/strips/pallas_call | solution.py:185
  163.7 4.6 %collective-permute-start.14 = (bf16[1600,128]{1,0:T(8,128)(2,1)S(1)}, bf16[1600,128]{1,0:T(8,128)(2,1)S(1)}, u32[]{:S(2)}, u32[]{:S(2)}) collective-permute-start(bf16[1600,128]{1,0:T(8,128)(2,1)S(1)} %collective-permute-done.12.part), channel_id=1, source_target_pairs={{0,15},{1,0},{2,1},{3,2},{4,3},{5,4},{6,5},{7,6},{8,7},{9,8},{10,9... | collective-permute-start | bytes 1228808 | tf_op jit(solution)/shard_map/ppermute | solution.py:331
  168.3 2.4 %strips.10._ = bf16[96,128,128]{2,1,0:T(8,128)(2,1)S(1)} custom-call(s32[8,128]{1,0:T(8,128)S(1)} %get-tuple-element.16.code_ref, bf16[1600,128]{1,0:T(8,128)(2,1)} %collective-permute-done.11.part, bf16[8,800,128]{2,1,0:T(8,128)(2,1)S(1)} %stack.1.mine_ref, ...), custom_call_target="tpu_custom_call", output_to_operand_aliasing={{}: (4, {})} | custom-call | tf_op jit(solution)/shard_map/strips/pallas_call | solution.py:185
  174.2 2.4 %strips.11._ = bf16[96,128,128]{2,1,0:T(8,128)(2,1)S(1)} custom-call(s32[8,128]{1,0:T(8,128)S(1)} %get-tuple-element.16.code_ref, bf16[1600,128]{1,0:T(8,128)(2,1)} %collective-permute-done.1.part, bf16[8,800,128]{2,1,0:T(8,128)(2,1)S(1)} %stack.1.mine_ref, ...), custom_call_target="tpu_custom_call", output_to_operand_aliasing={{}: (4, {})} | custom-call | tf_op jit(solution)/shard_map/strips/pallas_call | solution.py:185
  176.6 2.0 %strips.12._ = bf16[96,128,128]{2,1,0:T(8,128)(2,1)S(1)} custom-call(s32[8,128]{1,0:T(8,128)S(1)} %get-tuple-element.16.code_ref, bf16[1600,128]{1,0:T(8,128)(2,1)S(1)} %collective-permute-done.12.part, bf16[8,800,128]{2,1,0:T(8,128)(2,1)S(1)} %stack.1.mine_ref, ...), custom_call_target="tpu_custom_call", output_to_operand_aliasing={{}: (4, {})} | custom-call | tf_op jit(solution)/shard_map/strips/pallas_call | solution.py:185
  178.6 2.0 %strips.13._ = bf16[96,128,128]{2,1,0:T(8,128)(2,1)S(1)} custom-call(s32[8,128]{1,0:T(8,128)S(1)} %get-tuple-element.16.code_ref, bf16[1600,128]{1,0:T(8,128)(2,1)S(1)} %collective-permute-done.10.part, bf16[8,800,128]{2,1,0:T(8,128)(2,1)S(1)} %stack.1.mine_ref, ...), custom_call_target="tpu_custom_call", output_to_operand_aliasing={{}: (4, {})} | custom-call | tf_op jit(solution)/shard_map/strips/pallas_call | solution.py:185
  180.6 2.0 %strips.14.filled_ref = bf16[96,128,128]{2,1,0:T(8,128)(2,1)S(1)} custom-call(s32[8,128]{1,0:T(8,128)S(1)} %get-tuple-element.16.code_ref, bf16[1600,128]{1,0:T(8,128)(2,1)S(1)} %collective-permute-done.14.part, bf16[8,800,128]{2,1,0:T(8,128)(2,1)S(1)} %stack.1.mine_ref, ...), custom_call_target="tpu_custom_call", output_to_operand_aliasing={{}: (4, {})} | custom-call | tf_op jit(solution)/shard_map/strips/pallas_call | solution.py:185
  184.3 2.7 %strips.15 = bf16[96,128,128]{2,1,0:T(8,128)(2,1)} custom-call(s32[8,128]{1,0:T(8,128)S(1)} %get-tuple-element.16.code_ref, bf16[1600,128]{1,0:T(8,128)(2,1)S(1)} %collective-permute-done.13.part, bf16[8,800,128]{2,1,0:T(8,128)(2,1)S(1)} %stack.1.mine_ref, bf16[8,800,128]{2,1,0:T(8,128)(2,1)S(1)} %collective-permute-done.9.other_ref, ...), custom_call_target="tpu_custom_call", output_to_operand_aliasing={{}: (4, {})} | custom-call | tf_op jit(solution)/shard_map/strips/pallas_call | solution.py:185
  (33 shorter events, 23.4 us)
Async XLA Ops:
  0.6 1.0 copy-start.2
  2.0 145.3 %copy-start.3 = (s32[256]{0:T(256)S(1)}, s32[256]{0:T(256)}, u32[]{:S(2)}) copy-start(s32[256]{0:T(256)} %owner_ref.1) | copy-start | bytes 3076
  67.5 41.0 %all-to-all-start.1 = ((bf16[16,104,128]{2,1,0:T(8,128)(2,1)}), bf16[16,104,128]{2,1,0:T(8,128)(2,1)S(1)}, u32[]{:S(2)}, u32[]{:S(2)}) async-start(bf16[16,104,128]{2,1,0:T(8,128)(2,1)} %route.1), calls=%async_computation.1 | async-start | bytes 851968 | tf_op jit(solution)/shard_map/all_to_all | solution.py:272
  80.9 17.0 %collective-permute-start.2 = (bf16[800,128]{1,0:T(8,128)(2,1)S(1)}, bf16[800,128]{1,0:T(8,128)(2,1)S(1)}, u32[]{:S(2)}, u32[]{:S(2)}) collective-permute-start(bf16[800,128]{1,0:T(8,128)(2,1)S(1)} %get-tuple-element.17.refs_0_), channel_id=1, source_target_pairs={{0,32},{16,48},{32,64},{48,80},{64,96},{80,112},{96,128},{112,144}... | collective-permute-start | bytes 614408 | tf_op jit(solution)/shard_map/ppermute | solution.py:258
  84.2 15.6 %collective-permute-start.5 = (bf16[800,128]{1,0:T(8,128)(2,1)S(1)}, bf16[800,128]{1,0:T(8,128)(2,1)S(1)}, u32[]{:S(2)}, u32[]{:S(2)}) collective-permute-start(bf16[800,128]{1,0:T(8,128)(2,1)S(1)} %get-tuple-element.17.refs_0_), channel_id=1, source_target_pairs={{0,224},{16,240},{32,0},{48,16},{64,32},{80,48},{96,64},{112,80},{... | collective-permute-start | bytes 614408 | tf_op jit(solution)/shard_map/ppermute | solution.py:258
  97.8 8.8 %collective-permute-start.3 = (bf16[800,128]{1,0:T(8,128)(2,1)S(1)}, bf16[800,128]{1,0:T(8,128)(2,1)S(1)}, u32[]{:S(2)}, u32[]{:S(2)}) collective-permute-start(bf16[800,128]{1,0:T(8,128)(2,1)S(1)} %collective-permute-done.2.refs_1_), channel_id=1, source_target_pairs={{0,32},{16,48},{32,64},{48,80},{64,96},{80,112},{96,128},{112,144}... | collective-permute-start | bytes 614408 | tf_op jit(solution)/shard_map/ppermute | solution.py:258
  99.8 9.7 %collective-permute-start.6 = (bf16[800,128]{1,0:T(8,128)(2,1)S(1)}, bf16[800,128]{1,0:T(8,128)(2,1)S(1)}, u32[]{:S(2)}, u32[]{:S(2)}) collective-permute-start(bf16[800,128]{1,0:T(8,128)(2,1)S(1)} %collective-permute-done.5.refs_5_), channel_id=1, source_target_pairs={{0,224},{16,240},{32,0},{48,16},{64,32},{80,48},{96,64},{112,80},{... | collective-permute-start | bytes 614408 | tf_op jit(solution)/shard_map/ppermute | solution.py:258
  106.6 7.7 %collective-permute-start.4 = (bf16[800,128]{1,0:T(8,128)(2,1)S(1)}, bf16[800,128]{1,0:T(8,128)(2,1)S(1)}, u32[]{:S(2)}, u32[]{:S(2)}) collective-permute-start(bf16[800,128]{1,0:T(8,128)(2,1)S(1)} %collective-permute-done.3.refs_2_), channel_id=1, source_target_pairs={{0,32},{16,48},{32,64},{48,80},{64,96},{80,112},{96,128},{112,144}... | collective-permute-start | bytes 614408 | tf_op jit(solution)/shard_map/ppermute | solution.py:258
  108.6 13.5 %copy-start = (bf16[16,104,128]{2,1,0:T(8,128)(2,1)}, bf16[16,104,128]{2,1,0:T(8,128)(2,1)S(1)}, u32[]{:S(2)}) copy-start(bf16[16,104,128]{2,1,0:T(8,128)(2,1)S(1)} %all-to-all-done.1.got_ref) | copy-start | bytes 1277956
  114.4 7.7 %collective-permute-start.7 = (bf16[800,128]{1,0:T(8,128)(2,1)S(1)}, bf16[800,128]{1,0:T(8,128)(2,1)S(1)}, u32[]{:S(2)}, u32[]{:S(2)}) collective-permute-start(bf16[800,128]{1,0:T(8,128)(2,1)S(1)} %collective-permute-done.4.refs_3_), channel_id=1, source_target_pairs={{0,32},{16,48},{32,64},{48,80},{64,96},{80,112},{96,128},{112,144}... | collective-permute-start | bytes 614408 | tf_op jit(solution)/shard_map/ppermute | solution.py:258
  116.3 7.3 %collective-permute-start.8 = (bf16[800,128]{1,0:T(8,128)(2,1)S(1)}, bf16[800,128]{1,0:T(8,128)(2,1)S(1)}, u32[]{:S(2)}, u32[]{:S(2)}) collective-permute-start(bf16[800,128]{1,0:T(8,128)(2,1)S(1)} %collective-permute-done.6.refs_6_), channel_id=1, source_target_pairs={{0,224},{16,240},{32,0},{48,16},{64,32},{80,48},{96,64},{112,80},{... | collective-permute-start | bytes 614408 | tf_op jit(solution)/shard_map/ppermute | solution.py:258
  123.7 30.2 %collective-permute-start.9 = (bf16[8,800,128]{2,1,0:T(8,128)(2,1)S(1)}, bf16[8,800,128]{2,1,0:T(8,128)(2,1)S(1)}, u32[]{:S(2)}, u32[]{:S(2)}) collective-permute-start(bf16[8,800,128]{2,1,0:T(8,128)(2,1)S(1)} %stack.1.mine_ref), channel_id=1, source_target_pairs={{0,16},{16,0},{32,48},{48,32},{64,80},{80,64},{96,112},{112,96},{1... | collective-permute-start | bytes 4915208 | tf_op jit(solution)/shard_map/ppermute | solution.py:313
  129.8 15.7 %collective-permute-start = (bf16[1600,128]{1,0:T(8,128)(2,1)}, bf16[1600,128]{1,0:T(8,128)(2,1)}, u32[]{:S(2)}, u32[]{:S(2)}) collective-permute-start(bf16[1600,128]{1,0:T(8,128)(2,1)} %pack.1.part), channel_id=1, source_target_pairs={{0,1},{1,2},{2,3},{3,4},{4,5},{5,6},{6,7},{7,8},{8,9},{9,10},{10,1... | collective-permute-start | bytes 1228808 | tf_op jit(solution)/shard_map/ppermute | solution.py:285
  131.7 17.6 %collective-permute-start.11 = (bf16[1600,128]{1,0:T(8,128)(2,1)}, bf16[1600,128]{1,0:T(8,128)(2,1)}, u32[]{:S(2)}, u32[]{:S(2)}) collective-permute-start(bf16[1600,128]{1,0:T(8,128)(2,1)} %pack.1.part), channel_id=1, source_target_pairs={{0,15},{1,0},{2,1},{3,2},{4,3},{5,4},{6,5},{7,6},{8,7},{9,8},{10,9... | collective-permute-start | bytes 1228808 | tf_op jit(solution)/shard_map/ppermute | solution.py:286
  145.4 13.9 %collective-permute-start.1 = (bf16[1600,128]{1,0:T(8,128)(2,1)}, bf16[1600,128]{1,0:T(8,128)(2,1)}, u32[]{:S(2)}, u32[]{:S(2)}) collective-permute-start(bf16[1600,128]{1,0:T(8,128)(2,1)} %collective-permute-done.part), channel_id=1, source_target_pairs={{0,1},{1,2},{2,3},{3,4},{4,5},{5,6},{6,7},{7,8},{8,9},{9,10},{10,1... | collective-permute-start | bytes 1228808 | tf_op jit(solution)/shard_map/ppermute | solution.py:325
  147.5 1.0 copy-start.1
  149.3 14.3 %collective-permute-start.12 = (bf16[1600,128]{1,0:T(8,128)(2,1)}, bf16[1600,128]{1,0:T(8,128)(2,1)S(1)}, u32[]{:S(2)}, u32[]{:S(2)}) collective-permute-start(bf16[1600,128]{1,0:T(8,128)(2,1)} %collective-permute-done.11.part), channel_id=1, source_target_pairs={{0,15},{1,0},{2,1},{3,2},{4,3},{5,4},{6,5},{7,6},{8,7},{9,8},{10,9... | collective-permute-start | bytes 1228808 | tf_op jit(solution)/shard_map/ppermute | solution.py:331
  159.3 12.9 %collective-permute-start.10 = (bf16[1600,128]{1,0:T(8,128)(2,1)}, bf16[1600,128]{1,0:T(8,128)(2,1)S(1)}, u32[]{:S(2)}, u32[]{:S(2)}) collective-permute-start(bf16[1600,128]{1,0:T(8,128)(2,1)} %collective-permute-done.1.part), channel_id=1, source_target_pairs={{0,1},{1,2},{2,3},{3,4},{4,5},{5,6},{6,7},{7,8},{8,9},{9,10},{10,1... | collective-permute-start | bytes 1228808 | tf_op jit(solution)/shard_map/ppermute | solution.py:325
  163.7 16.9 %collective-permute-start.14 = (bf16[1600,128]{1,0:T(8,128)(2,1)S(1)}, bf16[1600,128]{1,0:T(8,128)(2,1)S(1)}, u32[]{:S(2)}, u32[]{:S(2)}) collective-permute-start(bf16[1600,128]{1,0:T(8,128)(2,1)S(1)} %collective-permute-done.12.part), channel_id=1, source_target_pairs={{0,15},{1,0},{2,1},{3,2},{4,3},{5,4},{6,5},{7,6},{8,7},{9,8},{10,9... | collective-permute-start | bytes 1228808 | tf_op jit(solution)/shard_map/ppermute | solution.py:331
  172.2 12.1 %collective-permute-start.13 = (bf16[1600,128]{1,0:T(8,128)(2,1)S(1)}, bf16[1600,128]{1,0:T(8,128)(2,1)S(1)}, u32[]{:S(2)}, u32[]{:S(2)}) collective-permute-start(bf16[1600,128]{1,0:T(8,128)(2,1)S(1)} %collective-permute-done.10.part), channel_id=1, source_target_pairs={{0,1},{1,2},{2,3},{3,4},{4,5},{5,6},{6,7},{7,8},{8,9},{9,10},{10,1... | collective-permute-start | bytes 1228808 | tf_op jit(solution)/shard_map/ppermute | solution.py:325
